TPU v7x, 32 devices: a whole 2x2x4 slice. The times are simulated.
32 devices in a mesh: aux: 4 (over z), orb: 8 (over y, x, core).
Axes of the slice: x: 2, y: 2, z: 4, core: 2. Of those that a mesh axis runs over, the one named last changes fastest.
Arguments:
- half: bfloat16 [64, 384, 3072], P('aux', 'orb'), may hold values from -1.25 to 1.25
- metric: bfloat16 [64, 64], P('aux'), may hold values from -1 to 2
- survive: int32 [4, 16, 24], P('aux', 'orb'), may hold values 0 or 1
Outputs:
- exchange_k: float32 [3072, 3072], P('orb', 'aux')
All inputs are finite; a program needn't handle non-finite values. No bound on the sum of `survive` on one device may be relied on, other than what follows from the above.
Results may differ from a plain program's by a relative error of at most 0.00098.
Values may be sent and summed in bfloat16 or wider, within the bound.
A program may use at most 128 MiB of HBM per device.

v0:
```python
import functools

import jax
import jax.numpy as jnp
from jax import lax
from jax.experimental import pallas as pl
from jax.experimental.pallas import tpu as pltpu
from jax.sharding import PartitionSpec as P

MESH = pl.DeviceIdType.MESH
F32 = jnp.float32


def gated(half, survive):
    aux_local, occ_local, ao_count = half.shape
    blocks_aux, blocks_occ, blocks_ao = survive.shape
    gate = survive.astype(jnp.bfloat16)
    shaped = half.reshape(
        blocks_aux, aux_local, blocks_occ, occ_local // blocks_occ, blocks_ao, ao_count // blocks_ao
    )
    return (shaped * gate[:, None, :, None, :, None]).reshape(aux_local, occ_local, ao_count)


def plain(half, metric, survive):
    aux_local, occ_local, ao_count = half.shape
    portion = lax.all_gather(gated(half, survive), "aux", axis=0, tiled=True)
    fit_total = jnp.dot(metric, portion.reshape(portion.shape[0], -1), preferred_element_type=F32)
    fitted = fit_total.astype(jnp.bfloat16).reshape(aux_local, occ_local, ao_count)
    group_width = ao_count // lax.axis_size("orb")
    row_start = lax.axis_index("orb") * group_width
    flat_rows = lax.all_gather(fitted, "orb", axis=1, tiled=True).reshape(-1, ao_count)
    left_rows = lax.dynamic_slice_in_dim(flat_rows, row_start, group_width, 1)
    partial_k = lax.dot_general(
        left_rows, flat_rows, (((0,), (0,)), ((), ())), preferred_element_type=F32
    )
    return lax.psum_scatter(partial_k, "aux", scatter_dimension=1, tiled=True)


def kernel(
    aux_local, m_ref, metric_ref, out_ref, held, fit, left, acc, peer, tile, via, last, whole, kron_ref,
    gs, gr, zs, zr, xs, xr, ys, yr, fs, fr, ps, pr, rs, rr,
):
    z = lax.axis_index("aux")
    orb = lax.axis_index("orb")
    n_aux = m_ref.shape[0]
    unit = m_ref.shape[1]
    ao = m_ref.shape[2]
    chip = orb // 2
    core = orb % 2
    pair_rows = acc.shape[0]
    rows = pair_rows // 2
    cols = out_ref.shape[1]
    half_rows = rows // 2
    x_peer = orb + 2 - 4 * (chip % 2)
    y_peer = orb + 4 - 8 * (chip // 2)
    partner = orb + 1 - 2 * core
    up, down, far = (z + 1) % n_aux, (z + n_aux - 1) % n_aux, (z + 2) % n_aux

    barrier = pltpu.get_barrier_semaphore()
    for a in (up, down, far):
        pl.semaphore_signal(barrier, inc=1, device_id={"aux": a, "orb": orb}, device_id_type=MESH)
    for o in (x_peer, y_peer, partner):
        pl.semaphore_signal(barrier, inc=1, device_id={"aux": z, "orb": o}, device_id_type=MESH)
    pl.semaphore_wait(barrier, 6)

    def remote(src, dst, send, recv, a, o):
        return pltpu.make_async_remote_copy(
            src_ref=src, dst_ref=dst, send_sem=send, recv_sem=recv,
            device_id={"aux": a, "orb": o}, device_id_type=MESH,
        )

    def span(s):
        return pl.ds(pl.multiple_of(s * unit, unit), unit)

    def source(d):
        return (z + n_aux - d) % n_aux

    metric_rows = pl.ds(pl.multiple_of(z * aux_local, aux_local), aux_local)
    gather = []
    for d in (1, 3, 2):
        copy = remote(metric_ref, whole.at[metric_rows], gs.at[d], gr.at[d], (z + d) % n_aux, orb)
        copy.start()
        gather.append(copy)
    spread = {}
    for d in (1, 3, 2):
        there = (z + d) % n_aux
        spread[d] = remote(m_ref.at[there], held.at[0, span(z)], zs.at[d], zr.at[d], there, orb)
        spread[d].start()

    to_x, to_y, onward = {}, {}, {}

    def share(d):
        own = span(source(d))
        if d:
            spread[d].wait_recv()
        block = held.at[0, own] if d else m_ref.at[z]
        to_x[d] = remote(block, held.at[1, own], xs.at[d], xr.at[d], z, x_peer)
        to_y[d] = remote(block, held.at[2, own], ys.at[d], yr.at[d], z, y_peer)
        to_x[d].start()
        to_y[d].start()

    def forward(d, from_x):
        own = span(source(d))
        if from_x:
            to_x[d].wait_recv()
            onward[d] = remote(held.at[1, own], held.at[3, own], fs.at[d], fr.at[d], z, y_peer)
        else:
            to_y[d].wait_recv()
            onward[d] = remote(held.at[2, own], held.at[3, own], fs.at[d], fr.at[d], z, x_peer)
        onward[d].start()

    step = 512
    mine = pl.ds(pl.multiple_of(chip * pair_rows, pair_rows), pair_rows)

    def contract(slot, first):
        @pl.loop(0, ao // step)
        def _(t):
            at = pl.ds(pl.multiple_of(t * step, step), step)
            fit[:, at] = jnp.dot(
                kron_ref[...], held[slot, :, at], preferred_element_type=F32
            ).astype(fit.dtype)

        left[...] = fit[:, mine].T

        @pl.loop(0, ao // step)
        def _(t):
            at = pl.ds(pl.multiple_of(t * step, step), step)
            more = jnp.dot(left[...], fit[:, at], preferred_element_type=F32)
            acc[:, at] = more if first else acc[:, at] + more

    def build_kron():
        whole[metric_rows, :] = metric_ref[...]
        for copy in gather:
            copy.wait_recv()
        depth, width = kron_ref.shape[0], whole.shape[1]

        def aux_of(r):
            return lax.div(r, unit) * aux_local + lax.rem(r, aux_local)

        def orbital_of(r):
            return lax.div(lax.rem(r, unit), aux_local)

        i32, bf16 = jnp.int32, kron_ref.dtype
        by_row = aux_of(lax.broadcasted_iota(i32, (width, depth), 1))
        pick = jnp.where(by_row == lax.broadcasted_iota(i32, (width, depth), 0), 1.0, 0.0)
        spread_cols = jnp.dot(whole[...], pick.astype(bf16), preferred_element_type=F32).astype(bf16)
        by_col = aux_of(lax.broadcasted_iota(i32, (depth, whole.shape[0]), 0))
        take = jnp.where(by_col == lax.broadcasted_iota(i32, (depth, whole.shape[0]), 1), 1.0, 0.0)
        both = jnp.dot(take.astype(bf16), spread_cols, preferred_element_type=F32)
        same = orbital_of(lax.broadcasted_iota(i32, (depth, depth), 0)) == orbital_of(
            lax.broadcasted_iota(i32, (depth, depth), 1)
        )
        kron_ref[...] = jnp.where(same, both, 0.0).astype(bf16)

    share(0)
    held[0, span(z), :] = m_ref[z]
    build_kron()
    share(1)
    share(3)
    forward(0, True)
    share(2)
    forward(1, False)
    contract(0, True)
    forward(3, True)
    to_x[1].wait_recv()
    to_x[2].wait_recv()
    contract(1, False)
    forward(2, False)
    to_y[0].wait_recv()
    to_y[3].wait_recv()
    contract(2, False)
    for d in range(4):
        onward[d].wait_recv()
    contract(3, False)

    def across(a):
        return pl.ds(pl.multiple_of(a * cols, cols), cols)

    my_rows = pl.ds(pl.multiple_of(core * rows, rows), rows)
    other_rows = pl.ds(pl.multiple_of((1 - core) * rows, rows), rows)
    order = (far, up, down, z)
    swaps = []
    for n, a in enumerate(order):
        swap = remote(acc.at[other_rows, across(a)], peer.at[n], ps.at[n], pr.at[n], z, partner)
        swap.start()
        swaps.append(swap)

    low, high = pl.ds(0, half_rows), pl.ds(half_rows, half_rows)

    def settle(n):
        swaps[n].wait_recv()
        tile[n] = acc[my_rows, across(order[n])] + peer[n]

    settle(0)
    far_up = remote(tile.at[0, low], via.at[0], rs.at[0], rr.at[0], up, orb)
    far_down = remote(tile.at[0, high], via.at[1], rs.at[1], rr.at[1], down, orb)
    far_up.start()
    far_down.start()
    settle(1)
    near_up = remote(tile.at[1, high], last.at[0, high], rs.at[2], rr.at[2], up, orb)
    near_up.start()
    settle(2)
    near_down = remote(tile.at[2, low], last.at[1, low], rs.at[3], rr.at[3], down, orb)
    near_down.start()
    settle(3)
    far_up.wait_recv()
    tile[1, low] += via[0]
    sum_up = remote(tile.at[1, low], last.at[0, low], rs.at[4], rr.at[4], up, orb)
    sum_up.start()
    far_down.wait_recv()
    tile[2, high] += via[1]
    sum_down = remote(tile.at[2, high], last.at[1, high], rs.at[5], rr.at[5], down, orb)
    sum_down.start()
    for copy in (near_up, near_down, sum_up, sum_down):
        copy.wait_recv()
    out_ref[...] = tile[3] + last[0] + last[1]
    for copy in (
        *gather, *spread.values(), *to_x.values(), *to_y.values(), *onward.values(), *swaps,
        far_up, far_down, near_up, near_down, sum_up, sum_down,
    ):
        copy.wait_send()


def direct(half, metric, survive):
    aux_local, occ_local, ao = half.shape
    n_aux, n_orb = lax.axis_size("aux"), lax.axis_size("orb")
    part = occ_local // n_aux
    blocks = gated(half, survive).transpose(1, 0, 2).reshape(n_aux, part * aux_local, ao)
    n_fit = n_aux * aux_local
    width = -(-n_fit // 128) * 128
    metric = jnp.pad(metric, ((0, 0), (0, width - n_fit)))
    depth = n_fit * part
    rows, cols = ao // n_orb, ao // n_aux
    dma = pltpu.SemaphoreType.DMA
    bf16 = jnp.bfloat16
    return pl.pallas_call(
        functools.partial(kernel, aux_local),
        out_shape=jax.ShapeDtypeStruct((rows, cols), F32),
        in_specs=[pl.BlockSpec(memory_space=pltpu.VMEM)] * 2,
        out_specs=pl.BlockSpec(memory_space=pltpu.VMEM),
        scratch_shapes=[
            pltpu.VMEM((4, depth, ao), bf16),
            pltpu.VMEM((depth, ao), bf16),
            pltpu.VMEM((2 * rows, depth), bf16),
            pltpu.VMEM((2 * rows, ao), F32),
            pltpu.VMEM((4, rows, cols), F32),
            pltpu.VMEM((4, rows, cols), F32),
            pltpu.VMEM((2, rows // 2, cols), F32),
            pltpu.VMEM((2, rows, cols), F32),
            pltpu.VMEM((n_fit, width), bf16),
            pltpu.VMEM((depth, depth), bf16),
        ]
        + [dma((4,))] * 12
        + [dma((6,))] * 2,
        compiler_params=pltpu.CompilerParams(
            collective_id=0, has_side_effects=True, vmem_limit_bytes=66 * 1000 * 1000
        ),
    )(blocks, metric)


def solution(mesh):
    square = mesh.shape["aux"] == 4 and mesh.shape["orb"] == 8
    return jax.shard_map(
        direct if square else plain,
        mesh=mesh,
        in_specs=(P("aux", "orb", None), P("aux", None), P("aux", "orb", None)),
        out_specs=P("orb", "aux"),
        check_vma=False,
    )
```

profile of v0, /device:TPU:0, one launch (start us, length us, event | category | flops | bytes accessed | tf_op | source)
XLA Modules:
  0.0 286.3 jit_solution(13193111221086492569)
XLA Ops:
  0.0 0.7 convert_bitcast_fusion
  0.7 0.1 mul.18
  0.8 2.8 multiply_bitcast_fusion
  3.7 0.0 copy-start
  3.7 4.7 %copy.4 = bf16[48,16,3072]{2,1,0:T(8,128)(2,1)} copy(bf16[48,16,3072]{2,0,1:T(8,128)(2,1)S(1)} %multiply_bitcast_fusion) | data formatting | bytes 9437184 | tf_op jit(solution)/shard_map/transpose | solution.py:228
  8.4 0.0 copy-done
  8.4 0.6 pad.4.metric_ref
  9.0 274.9 %shard_map.37 = f32[384,768]{1,0:T(8,128)} custom-call(bf16[4,192,3072]{2,1,0:T(8,128)(2,1)} %bitcast.10, bf16[16,128]{1,0:T(8,128)(2,1)} %pad.4.metric_ref), custom_call_target="tpu_custom_call" | custom-call | tf_op jit(solution)/shard_map/pallas_call | solution.py:236
  283.9 2.4 copy.9
  (1 shorter events, 0.0 us)
Async XLA Ops:
  3.7 4.7 %copy-start = (bf16[16,64]{1,0:T(8,128)(2,1)S(1)}, bf16[16,64]{1,0:T(8,128)(2,1)}, u32[]{:S(2)}) copy-start(bf16[16,64]{1,0:T(8,128)(2,1)} %param.4) | copy-start | bytes 6148
where the time goes:
time: 288 us; the launch traced here: 286 us
  Pallas kernels  275 us (95%)
  local copies, waits for them, and re-layouts  7.82 us (3%)
  other arithmetic  3.48 us (1%)
    pallas_call x1, Pallas kernels, direct(): pl.pallas_call(functools.partial(kernel, aux_local), out_shape=jax.ShapeD...  275 us

commit v1 on v0

v1 whole, which is shorter than its diff:
```python
import functools

import jax
import jax.numpy as jnp
from jax import lax
from jax.experimental import pallas as pl
from jax.experimental.pallas import tpu as pltpu
from jax.sharding import PartitionSpec as P

MESH = pl.DeviceIdType.MESH
F32 = jnp.float32


def gated(half, survive):
    aux_local, occ_local, ao_count = half.shape
    blocks_aux, blocks_occ, blocks_ao = survive.shape
    gate = survive.astype(jnp.bfloat16)
    shaped = half.reshape(
        blocks_aux, aux_local, blocks_occ, occ_local // blocks_occ, blocks_ao, ao_count // blocks_ao
    )
    return (shaped * gate[:, None, :, None, :, None]).reshape(aux_local, occ_local, ao_count)


def plain(half, metric, survive):
    aux_local, occ_local, ao_count = half.shape
    portion = lax.all_gather(gated(half, survive), "aux", axis=0, tiled=True)
    fit_total = jnp.dot(metric, portion.reshape(portion.shape[0], -1), preferred_element_type=F32)
    fitted = fit_total.astype(jnp.bfloat16).reshape(aux_local, occ_local, ao_count)
    group_width = ao_count // lax.axis_size("orb")
    row_start = lax.axis_index("orb") * group_width
    flat_rows = lax.all_gather(fitted, "orb", axis=1, tiled=True).reshape(-1, ao_count)
    left_rows = lax.dynamic_slice_in_dim(flat_rows, row_start, group_width, 1)
    partial_k = lax.dot_general(
        left_rows, flat_rows, (((0,), (0,)), ((), ())), preferred_element_type=F32
    )
    return lax.psum_scatter(partial_k, "aux", scatter_dimension=1, tiled=True)

TOP = 32000.0
FINE = 256.0


def kernel(
    aux_local, m_ref, metric_ref, out_ref, held, fit, left, acc, whole, kron_ref,
    rs_out, rs_in, z_out, z_in, swap_out, swap_in,
    gs, gr, zs, zr, fs, fr, rs, rr, cs, cr, ws, wr,
):
    z = lax.axis_index("aux")
    orb = lax.axis_index("orb")
    n_aux = m_ref.shape[0]
    parts = held.shape[1]
    unit = m_ref.shape[1] // parts
    panel = acc.shape[1]
    width = acc.shape[2]
    piece = width // n_aux
    chip = orb // 2
    core = orb % 2
    x_chip = chip + 1 - 2 * (chip % 2)
    y_chip = chip + 2 - 4 * (chip // 2)
    partner = orb + 1 - 2 * core
    other_chip = core * x_chip + (1 - core) * y_chip
    rs_peer = 2 * other_chip + core
    side = z // 2
    mate = z + 1 - 2 * (z % 2)
    far_inner = 2 - side
    far_end = 3 - 3 * side
    inner = (z + 1) // 2 % 2 == 1

    barrier = pltpu.get_barrier_semaphore()
    for d in (1, 2, 3):
        pl.semaphore_signal(
            barrier, inc=1, device_id={"aux": (z + d) % n_aux, "orb": orb}, device_id_type=MESH
        )
    near = (partner, 2 * x_chip, 2 * x_chip + 1, 2 * y_chip, 2 * y_chip + 1)
    for o in near:
        pl.semaphore_signal(barrier, inc=1, device_id={"aux": z, "orb": o}, device_id_type=MESH)
    pl.semaphore_wait(barrier, 8)

    def remote(src, dst, send, recv, a, o):
        return pltpu.make_async_remote_copy(
            src_ref=src, dst_ref=dst, send_sem=send, recv_sem=recv,
            device_id={"aux": a, "orb": o}, device_id_type=MESH,
        )

    def span(s):
        return pl.ds(pl.multiple_of(s * unit, unit), unit)

    first = 1 + z % 2
    third = 3 - 3 * side
    second = 6 - first - third - z
    spread = []
    for s, there in enumerate((first, second, third)):
        for q in range(parts):
            copy = remote(
                m_ref.at[there, pl.ds(q * unit, unit)], held.at[0, q, span(z)],
                zs.at[s * parts + q], zr.at[z * parts + q], there, orb,
            )
            copy.start()
            spread.append(copy)

    shared = []

    def share(source, r, q, block):
        n = r * parts + q
        targets = ((1, partner), (2 + core, 2 * x_chip), (2 + core, 2 * y_chip + 1))
        for k, (slot, o) in enumerate(targets):
            copy = remote(
                block, held.at[slot, q, span(source)], fs.at[k * 4 * parts + n],
                fr.at[slot * 4 * parts + n], z, o,
            )
            copy.start()
            shared.append(copy)

    sources = (z, mate, far_inner, far_end)

    def arrive(r, q):
        source = sources[r]
        here = held.at[0, q, span(source)]
        remote(here, here, zs.at[q], zr.at[source * parts + q], mate, orb).wait_recv()
        share(source, r, q, here)

    for q in range(parts):
        share(z, 0, q, m_ref.at[z, pl.ds(q * unit, unit)])
    metric_rows = pl.ds(pl.multiple_of(z * aux_local, aux_local), aux_local)
    gather = []
    for d in (1, 3, 2):
        copy = remote(metric_ref, whole.at[metric_rows], gs.at[d], gr.at[d], (z + d) % n_aux, orb)
        copy.start()
        gather.append(copy)

    def build_kron():
        whole[metric_rows, :] = metric_ref[...]
        for copy in gather:
            copy.wait_recv()
        depth, wide = kron_ref.shape[0], whole.shape[1]

        def aux_of(r):
            return lax.div(r, unit) * aux_local + lax.rem(r, aux_local)

        def orbital_of(r):
            return lax.div(lax.rem(r, unit), aux_local)

        i32, bf16 = jnp.int32, kron_ref.dtype
        by_row = aux_of(lax.broadcasted_iota(i32, (wide, depth), 1))
        pick = jnp.where(by_row == lax.broadcasted_iota(i32, (wide, depth), 0), 1.0, 0.0)
        spread_cols = jnp.dot(whole[...], pick.astype(bf16), preferred_element_type=F32).astype(bf16)
        by_col = aux_of(lax.broadcasted_iota(i32, (depth, whole.shape[0]), 0))
        take = jnp.where(by_col == lax.broadcasted_iota(i32, (depth, whole.shape[0]), 1), 1.0, 0.0)
        both = jnp.dot(take.astype(bf16), spread_cols, preferred_element_type=F32)
        same = orbital_of(lax.broadcasted_iota(i32, (depth, depth), 0)) == orbital_of(
            lax.broadcasted_iota(i32, (depth, depth), 1)
        )
        kron_ref[...] = jnp.where(same, both, 0.0).astype(bf16)

    slab = kron_ref.shape[0]

    def aligned(start, size, unit_of=128):
        return pl.ds(pl.multiple_of(start, unit_of), size)

    def fit_part(q):
        @pl.loop(0, 4)
        def _(slot):
            rows = aligned(slot * slab, slab)

            def put(at, columns):
                fit[rows, at] = jnp.dot(
                    kron_ref[...], held[slot, q, :, columns], preferred_element_type=F32
                ).astype(fit.dtype)

            for b in range(n_aux):
                put(pl.ds(b * piece, piece), aligned((2 * b + core) * piece, piece))
            put(pl.ds(width, panel), aligned(chip * panel, panel))
            put(pl.ds(width + panel, panel), aligned(other_chip * panel, panel))

        left[0] = fit[:, width : width + panel].T
        left[1] = fit[:, width + panel :].T

    def contract(p, start, size, begin):
        at = aligned(start, size)
        more = jnp.dot(left[p], fit[:, at], preferred_element_type=F32)
        acc[p, :, at] = more if begin else acc[p, :, at] + more

    def contract_all(begin):
        step = 512

        @pl.loop(0, width // step)
        def _(t):
            contract(0, t * step, step, begin)
            contract(1, t * step, step, begin)

    strip = 64

    def block_at(b):
        return aligned(b * piece, piece)

    def quantize(p, b, target):
        at = block_at(b)

        def tops(t, top):
            rows = acc[p, aligned(t * strip, strip, strip), at]
            return jnp.maximum(top, jnp.max(jnp.abs(rows).reshape(strip // 8, 8, piece), axis=0))

        top = lax.fori_loop(0, panel // strip, tops, jnp.zeros((8, piece), F32))
        top = jnp.maximum(jnp.max(top, axis=0, keepdims=True), 1e-30)
        level = jnp.ceil(jnp.log2(top) * FINE)
        scale = TOP * jnp.exp2(level * (-1.0 / FINE))

        @pl.loop(0, panel // strip)
        def _(t):
            rows = aligned(t * strip, strip, strip)
            target[rows, :] = jnp.round(acc[p, rows, at] * scale).astype(jnp.int32).astype(jnp.int16)

        target[pl.ds(panel, 16), :] = jnp.broadcast_to(
            level.astype(jnp.int32), (16, piece)
        ).astype(jnp.int16)

    def add_in(source, b):
        at = block_at(b)
        level = source[pl.ds(panel, 16), :].astype(F32)[:1]
        scale = jnp.exp2(level * (1.0 / FINE)) * (1.0 / TOP)

        @pl.loop(0, panel // strip)
        def _(t):
            rows = aligned(t * strip, strip, strip)
            acc[0, rows, at] = acc[0, rows, at] + source[rows, :].astype(F32) * scale

    def slots_of(q):
        for slot in (1, 2, 3):
            for r in range(4):
                here = held.at[slot, q, span(sources[r])]
                remote(
                    here, here, fs.at[0], fr.at[slot * 4 * parts + r * parts + q], z, partner
                ).wait_recv()

    held_own = [(q, q * unit) for q in range(parts)]
    for q, at in held_own:
        held[0, q, span(z), :] = m_ref[z, pl.ds(at, unit), :]
    build_kron()
    for r in (1, 2):
        for q in range(parts):
            arrive(r, q)
    arrive(3, 0)
    arrive(3, 1)
    slots_of(0)
    fit_part(0)
    contract_all(True)
    arrive(3, 2)
    slots_of(1)
    fit_part(1)
    contract_all(False)
    slots_of(2)
    fit_part(2)

    order = (far_inner, far_end, mate, z)
    far_half, near_half = (1 - side) * 2 * piece, side * 2 * piece
    reduce_copies = []

    def give(n):
        quantize(1, order[n], rs_out.at[n])
        copy = remote(rs_out.at[n], rs_in.at[n], rs.at[n], rr.at[n], z, rs_peer)
        copy.start()
        reduce_copies.append(copy)

    contract(1, far_half, 2 * piece, False)
    give(0)
    give(1)
    contract(1, near_half, 2 * piece, False)
    give(2)
    give(3)
    contract(0, far_half, 2 * piece, False)
    contract(0, near_half, 2 * piece, False)

    def along(n, there, into):
        return remote(z_out.at[n], z_in.at[into], cs.at[n], cr.at[into], there, orb)

    up_to_mate = (along(0, mate, 0), along(1, mate, 1))
    to_mate = along(2, mate, 2)
    across = (along(0, far_inner, 3), along(1, far_end, 3))
    for n in (0, 1):
        reduce_copies[n].wait_recv()
        add_in(rs_in.at[n], order[n])

        @pl.when(jnp.logical_not(inner))
        def _():
            quantize(0, order[n], z_out.at[n])
            up_to_mate[n].start()

    reduce_copies[2].wait_recv()
    add_in(rs_in.at[2], mate)
    quantize(0, mate, z_out.at[2])
    to_mate.start()
    reduce_copies[3].wait_recv()
    add_in(rs_in.at[3], z)

    @pl.when(inner)
    def _():
        for n in (0, 1):
            up_to_mate[n].wait_recv()
            add_in(z_in.at[n], order[n])
            quantize(0, order[n], z_out.at[n])
            across[n].start()

    to_mate.wait_recv()
    add_in(z_in.at[2], z)
    across[0].wait_recv()
    add_in(z_in.at[3], z)
    rows = out_ref.shape[0]
    own_at = block_at(z)
    swap_out[...] = acc[0, aligned((1 - core) * rows, rows), own_at]
    swap = remote(swap_out, swap_in, ws.at[0], wr.at[0], z, partner)
    swap.start()
    out_ref[:, aligned(core * piece, piece)] = acc[0, aligned(core * rows, rows), own_at]
    swap.wait_recv()
    out_ref[:, aligned((1 - core) * piece, piece)] = swap_in[...]

    @pl.when(inner)
    def _():
        for copy in across:
            copy.wait_send()

    @pl.when(jnp.logical_not(inner))
    def _():
        for copy in up_to_mate:
            copy.wait_send()

    for copy in (*gather, *spread, *shared, *reduce_copies, to_mate, swap):
        copy.wait_send()


def direct(half, metric, survive):
    aux_local, occ_local, ao = half.shape
    n_aux, n_orb = lax.axis_size("aux"), lax.axis_size("orb")
    part = occ_local // n_aux
    blocks = gated(half, survive).transpose(1, 0, 2).reshape(n_aux, part * aux_local, ao)
    n_fit = n_aux * aux_local
    width = -(-n_fit // 128) * 128
    metric = jnp.pad(metric, ((0, 0), (0, width - n_fit)))
    parts = 3
    slab = n_fit * part // parts
    rows, cols = ao // n_orb, ao // n_aux
    panel, half_width = 2 * rows, ao // 2
    piece = half_width // n_aux
    dma = pltpu.SemaphoreType.DMA
    bf16, i16 = jnp.bfloat16, jnp.int16
    return pl.pallas_call(
        functools.partial(kernel, aux_local),
        out_shape=jax.ShapeDtypeStruct((rows, cols), F32),
        in_specs=[pl.BlockSpec(memory_space=pltpu.VMEM)] * 2,
        out_specs=pl.BlockSpec(memory_space=pltpu.VMEM),
        scratch_shapes=[
            pltpu.VMEM((4, parts, slab, ao), bf16),
            pltpu.VMEM((4 * slab, half_width + 2 * panel), bf16),
            pltpu.VMEM((2, panel, 4 * slab), bf16),
            pltpu.VMEM((2, panel, half_width), F32),
            pltpu.VMEM((n_fit, width), bf16),
            pltpu.VMEM((slab, slab), bf16),
            pltpu.VMEM((4, panel + 16, piece), i16),
            pltpu.VMEM((4, panel + 16, piece), i16),
            pltpu.VMEM((3, panel + 16, piece), i16),
            pltpu.VMEM((4, panel + 16, piece), i16),
            pltpu.VMEM((rows, piece), F32),
            pltpu.VMEM((rows, piece), F32),
            dma((4,)), dma((4,)),
            dma((3 * parts,)), dma((n_aux * parts,)),
            dma((12 * parts,)), dma((16 * parts,)),
            dma((4,)), dma((4,)),
            dma((3,)), dma((4,)),
            dma((1,)), dma((1,)),
        ],
        compiler_params=pltpu.CompilerParams(
            collective_id=0, has_side_effects=True, vmem_limit_bytes=66 * 1000 * 1000
        ),
    )(blocks, metric)


def solution(mesh):
    square = mesh.shape["aux"] == 4 and mesh.shape["orb"] == 8
    return jax.shard_map(
        direct if square else plain,
        mesh=mesh,
        in_specs=(P("aux", "orb", None), P("aux", None), P("aux", "orb", None)),
        out_specs=P("orb", "aux"),
        check_vma=False,
    )
```

time: 288 us -> 269 us (0.934)
  Pallas kernels: 275 us -> 257 us
    pallas_call x1, Pallas kernels: 275 us -> 257 us  [direct(): pl.pallas_call(functools.partial(kernel, aux_local), out_shape=jax.ShapeD...]
where the time goes in v1:
time: 269 us; the launch traced here: 268 us
  Pallas kernels  257 us (96%)
  local copies, waits for them, and re-layouts  7.82 us (3%)
  other arithmetic  3.48 us (1%)
    pallas_call x1, Pallas kernels, direct(): pl.pallas_call(functools.partial(kernel, aux_local), out_shape=jax.ShapeD...  257 us

profile of v1, /device:TPU:0, one launch (start us, length us, event | category | flops | bytes accessed | tf_op | source)
XLA Modules:
  0.0 268.5 jit_solution(8844987777416281520)
XLA Ops:
  0.0 0.7 convert_bitcast_fusion
  0.7 0.1 mul.18
  0.8 2.8 %multiply_bitcast_fusion = bf16[48,16,3072]{2,0,1:T(8,128)(2,1)S(1)} fusion(bf16[16,48,3072]{2,1,0:T(8,128)(2,1)} %param.3, bf16[48,3072]{1,0:T(8,128)(2,1)S(1)} %bitcast.11), kind=kLoop, calls=%fused_computation | loop fusion | flops 2359296 | bytes 9732096 | tf_op jit(solution)/shard_map/transpose | solution.py:333
  3.7 0.0 copy-start
  3.7 4.7 %copy.4 = bf16[48,16,3072]{2,1,0:T(8,128)(2,1)} copy(bf16[48,16,3072]{2,0,1:T(8,128)(2,1)S(1)} %multiply_bitcast_fusion) | data formatting | bytes 9437184 | tf_op jit(solution)/shard_map/transpose | solution.py:333
  8.4 0.0 copy-done
  8.4 0.6 pad.4.metric_ref
  9.0 257.1 %shard_map.37 = f32[384,768]{1,0:T(8,128)} custom-call(bf16[4,192,3072]{2,1,0:T(8,128)(2,1)} %bitcast.10, bf16[16,128]{1,0:T(8,128)(2,1)} %pad.4.metric_ref), custom_call_target="tpu_custom_call" | custom-call | tf_op jit(solution)/shard_map/pallas_call | solution.py:344
  266.1 2.4 copy.9
  (1 shorter events, 0.0 us)
Async XLA Ops:
  3.7 4.7 %copy-start = (bf16[16,64]{1,0:T(8,128)(2,1)S(1)}, bf16[16,64]{1,0:T(8,128)(2,1)}, u32[]{:S(2)}) copy-start(bf16[16,64]{1,0:T(8,128)(2,1)} %param.4) | copy-start | bytes 6148

commit v2 on v1

v2 whole, which is shorter than its diff:
```python
import functools

import jax
import jax.numpy as jnp
from jax import lax
from jax.experimental import pallas as pl
from jax.experimental.pallas import tpu as pltpu
from jax.sharding import PartitionSpec as P

MESH = pl.DeviceIdType.MESH
F32 = jnp.float32


def gated(half, survive):
    aux_local, occ_local, ao_count = half.shape
    blocks_aux, blocks_occ, blocks_ao = survive.shape
    gate = survive.astype(jnp.bfloat16)
    shaped = half.reshape(
        blocks_aux, aux_local, blocks_occ, occ_local // blocks_occ, blocks_ao, ao_count // blocks_ao
    )
    return (shaped * gate[:, None, :, None, :, None]).reshape(aux_local, occ_local, ao_count)


def plain(half, metric, survive):
    aux_local, occ_local, ao_count = half.shape
    portion = lax.all_gather(gated(half, survive), "aux", axis=0, tiled=True)
    fit_total = jnp.dot(metric, portion.reshape(portion.shape[0], -1), preferred_element_type=F32)
    fitted = fit_total.astype(jnp.bfloat16).reshape(aux_local, occ_local, ao_count)
    group_width = ao_count // lax.axis_size("orb")
    row_start = lax.axis_index("orb") * group_width
    flat_rows = lax.all_gather(fitted, "orb", axis=1, tiled=True).reshape(-1, ao_count)
    left_rows = lax.dynamic_slice_in_dim(flat_rows, row_start, group_width, 1)
    partial_k = lax.dot_general(
        left_rows, flat_rows, (((0,), (0,)), ((), ())), preferred_element_type=F32
    )
    return lax.psum_scatter(partial_k, "aux", scatter_dimension=1, tiled=True)

TOP = 32000.0
FINE = 256.0


def kernel(
    aux_local, m_ref, metric_ref, out_ref, held, fit, left, acc, whole, kron_ref,
    rs_out, rs_in, z_out, z_in,
    gs, gr, zs, zr, fs, fr, rs, rr, cs, cr, ws, wr,
):
    z = lax.axis_index("aux")
    orb = lax.axis_index("orb")
    n_aux = m_ref.shape[0]
    parts = held.shape[1]
    unit = m_ref.shape[1] // parts
    panel = acc.shape[1]
    rows = panel // 2
    slab = kron_ref.shape[0]
    chip = orb // 2
    core = orb % 2
    x, y = chip % 2, chip // 2
    x_chip = chip + 1 - 2 * x
    y_chip = chip + 2 - 4 * y
    partner = orb + 1 - 2 * core
    other_chip = core * x_chip + (1 - core) * y_chip
    rs_peer = 2 * other_chip + core
    unused = core * (3 - 3 * y) + (1 - core) * (1 + x)
    third = 6 - unused - chip - other_chip
    side = z // 2
    end = z % 3 == 0
    mate = z + 1 - 2 * (z % 2)
    near_block = core * (1 + side) + (1 - core) * 3 * side
    far_block = 3 - near_block
    holder = near_block == z

    barrier = pltpu.get_barrier_semaphore()
    for d in (1, 2, 3):
        pl.semaphore_signal(
            barrier, inc=1, device_id={"aux": (z + d) % n_aux, "orb": orb}, device_id_type=MESH
        )
    for o in (partner, 2 * x_chip, 2 * x_chip + 1, 2 * y_chip, 2 * y_chip + 1):
        pl.semaphore_signal(barrier, inc=1, device_id={"aux": z, "orb": o}, device_id_type=MESH)
    pl.semaphore_wait(barrier, 8)

    def remote(src, dst, send, recv, a, o):
        return pltpu.make_async_remote_copy(
            src_ref=src, dst_ref=dst, send_sem=send, recv_sem=recv,
            device_id={"aux": a, "orb": o}, device_id_type=MESH,
        )

    def aligned(start, size, unit_of=128):
        return pl.ds(pl.multiple_of(start, unit_of), size)

    def span(s):
        return aligned(s * unit, unit, unit)

    metric_rows = aligned(z * aux_local, aux_local, aux_local)
    gather = []
    for d in (1, 3, 2):
        copy = remote(metric_ref, whole.at[metric_rows], gs.at[d], gr.at[d], (z + d) % n_aux, orb)
        copy.start()
        gather.append(copy)

    spread = []
    there_last = 2 - z - z % 2 + 3 * side
    for s, there in enumerate((3 - 3 * side, 1 + z % 2, there_last)):
        for q in range(parts):
            copy = remote(
                m_ref.at[there, pl.ds(q * unit, unit)], held.at[0, q, span(z)],
                zs.at[s * parts + q], zr.at[z * parts + q], there, orb,
            )
            copy.start()
            spread.append(copy)

    sources = (z, 3 - 3 * (z % 2), (z + 2) % n_aux, 1 + z % 2)
    shared = []

    def recv_at(slot, r, q, k):
        return fr.at[((slot * 4 + r) * parts + q) * 2 + k]

    def share(r, q, whole_block, cut):
        source = sources[r]
        jobs = [(whole_block, partner, 1, pl.ds(0, 4 * panel), 0)]
        for o, slot, first, pair in (
            (2 * x_chip, 2 + core, 3 - 3 * x, 2 * x),
            (2 * y_chip + 1, 2 + core, 1 - y, 2 - y),
        ):
            one, two = aligned(first * panel, panel), aligned(pair * panel, 2 * panel)
            jobs += [(cut(one), o, slot, one, 0), (cut(two), o, slot, two, 1)]
        for n, (block, o, slot, columns, k) in enumerate(jobs):
            copy = remote(
                block, held.at[slot, q, span(source), columns],
                fs.at[(n * 4 + r) * parts + q], recv_at(slot, r, q, k), z, o,
            )
            copy.start()
            shared.append(copy)

    def arrive(r, q):
        at = span(sources[r])
        here = held.at[0, q, at]
        remote(here, here, zs.at[q], zr.at[sources[r] * parts + q], mate, orb).wait_recv()
        share(r, q, here, lambda columns: held.at[0, q, at, columns])

    def share_own(q):
        at = pl.ds(q * unit, unit)
        share(0, q, m_ref.at[z, at], lambda columns: m_ref.at[z, at, columns])

    for q in range(parts):
        share_own(q)

    def build_kron():
        whole[metric_rows, :] = metric_ref[...]
        for copy in gather:
            copy.wait_recv()
        depth, wide = kron_ref.shape[0], whole.shape[1]

        def aux_of(r):
            return lax.div(r, unit) * aux_local + lax.rem(r, aux_local)

        def orbital_of(r):
            return lax.div(lax.rem(r, unit), aux_local)

        i32, bf16 = jnp.int32, kron_ref.dtype
        by_row = aux_of(lax.broadcasted_iota(i32, (wide, depth), 1))
        pick = jnp.where(by_row == lax.broadcasted_iota(i32, (wide, depth), 0), 1.0, 0.0)
        spread_cols = jnp.dot(whole[...], pick.astype(bf16), preferred_element_type=F32).astype(bf16)
        by_col = aux_of(lax.broadcasted_iota(i32, (depth, whole.shape[0]), 0))
        take = jnp.where(by_col == lax.broadcasted_iota(i32, (depth, whole.shape[0]), 1), 1.0, 0.0)
        both = jnp.dot(take.astype(bf16), spread_cols, preferred_element_type=F32)
        same = orbital_of(lax.broadcasted_iota(i32, (depth, depth), 0)) == orbital_of(
            lax.broadcasted_iota(i32, (depth, depth), 1)
        )
        kron_ref[...] = jnp.where(same, both, 0.0).astype(bf16)

    def slots_of(q):
        first = core * y + (1 - core) * 3 * x
        pair = core * (1 + y) + (1 - core) * 2 * (1 - x)
        one, two = aligned(first * panel, panel), aligned(pair * panel, 2 * panel)
        for r in range(4):
            at = span(sources[r])
            for slot, k, columns in (
                (1, 0, pl.ds(0, 4 * panel)), (2, 0, one), (2, 1, two), (3, 0, one), (3, 1, two)
            ):
                here = held.at[slot, q, at, columns]
                remote(here, here, fs.at[0], recv_at(slot, r, q, k), z, partner).wait_recv()

    def fit_part(q):
        @pl.loop(0, 4)
        def _(slot):
            for n, p in enumerate((chip, other_chip, third)):
                fit[aligned(slot * slab, slab, slab), pl.ds(n * panel, panel)] = jnp.dot(
                    kron_ref[...], held[slot, q, :, aligned(p * panel, panel)],
                    preferred_element_type=F32,
                ).astype(fit.dtype)

        for n in range(2):
            left[n] = fit[:, n * panel : (n + 1) * panel].T

    def place(block):
        return jnp.where(block == chip, 0, jnp.where(block == other_chip, 1, 2))

    near, far = (near_block, side), (far_block, 1 - side)

    def block_at(block):
        return aligned(block[1] * panel, panel)

    def contract(p, block, begin):
        columns = fit[:, aligned(place(block[0]) * panel, panel)]
        at = block_at(block)
        more = jnp.dot(left[p], columns, preferred_element_type=F32)
        acc[p, :, at] = more if begin else acc[p, :, at] + more

    def contract_all(begin):
        for p in range(2):
            contract(p, far, begin)
            contract(p, near, begin)

    strip = 32
    halves = (1 - core, core)

    def quantize(p, block, h, target):
        at = block_at(block)

        def tops(t, top):
            some = acc[p, aligned(h * rows + t * strip, strip, strip), at]
            return jnp.maximum(top, jnp.max(jnp.abs(some).reshape(strip // 8, 8, panel), axis=0))

        top = lax.fori_loop(0, rows // strip, tops, jnp.zeros((8, panel), F32))
        top = jnp.maximum(jnp.max(top, axis=0, keepdims=True), 1e-30)
        level = jnp.ceil(jnp.log2(top) * FINE)
        scale = TOP * jnp.exp2(level * (-1.0 / FINE))

        @pl.loop(0, rows // strip)
        def _(t):
            some = acc[p, aligned(h * rows + t * strip, strip, strip), at]
            target[aligned(t * strip, strip, strip), :] = (
                jnp.round(some * scale).astype(jnp.int32).astype(jnp.int16)
            )

        target[pl.ds(rows, 16), :] = jnp.broadcast_to(
            level.astype(jnp.int32), (16, panel)
        ).astype(jnp.int16)

    def add_in(source, block, h):
        at = block_at(block)
        level = source[pl.ds(rows, 16), :].astype(F32)[:1]
        scale = jnp.exp2(level * (1.0 / FINE)) * (1.0 / TOP)

        @pl.loop(0, rows // strip)
        def _(t):
            here = aligned(h * rows + t * strip, strip, strip)
            some = source[aligned(t * strip, strip, strip), :].astype(F32)
            acc[0, here, at] = acc[0, here, at] + some * scale

    for q in range(parts):
        held[0, q, span(z), :] = m_ref[z, pl.ds(q * unit, unit), :]
    build_kron()
    for r in (1, 2):
        for q in range(parts):
            arrive(r, q)
    arrive(3, 0)
    arrive(3, 1)
    slots_of(0)
    fit_part(0)
    contract_all(True)
    arrive(3, 2)
    slots_of(1)
    fit_part(1)
    contract_all(False)
    slots_of(2)
    fit_part(2)

    given = []

    def give(block, n):
        for i, h in enumerate(halves):
            slot = 2 * n + i
            quantize(1, block, h, rs_out.at[slot])
            copy = remote(rs_out.at[slot], rs_in.at[slot], rs.at[slot], rr.at[slot], z, rs_peer)
            copy.start()
            given.append(copy)

    contract(1, far, False)
    give(far, 0)
    contract(1, near, False)
    give(near, 1)
    contract(0, far, False)
    contract(0, near, False)

    def along(n, into, there):
        return remote(z_out.at[n], z_in.at[into], cs.at[n], cr.at[into], there, orb)

    inward = [along(i, i, mate) for i in range(2)]
    to_mate = [along(2 + i, 2 + i, mate) for i in range(2)]
    across = [along(i, 4 + i, far_block) for i in range(2)]
    for i, h in enumerate(halves):
        given[i].wait_recv()
        add_in(rs_in.at[i], far, h)

        @pl.when(end)
        def _():
            quantize(0, far, h, z_out.at[i])
            inward[i].start()

    for i, h in enumerate(halves):
        given[2 + i].wait_recv()
        add_in(rs_in.at[2 + i], near, h)

        @pl.when(jnp.logical_not(holder))
        def _():
            quantize(0, near, h, z_out.at[2 + i])
            to_mate[i].start()

    @pl.when(jnp.logical_not(end))
    def _():
        for i, h in enumerate(halves):
            inward[i].wait_recv()
            add_in(z_in.at[i], far, h)
            quantize(0, far, h, z_out.at[i])
            across[i].start()

    own_at = block_at(near)
    last = remote(
        acc.at[0, aligned((1 - core) * rows, rows, rows), own_at], out_ref,
        ws.at[0], wr.at[0], z, partner,
    )

    @pl.when(holder)
    def _():
        for i, h in enumerate(halves):
            to_mate[i].wait_recv()
            add_in(z_in.at[2 + i], near, h)
        for i, h in enumerate(halves):
            across[i].wait_recv()
            add_in(z_in.at[4 + i], near, h)
            if i == 0:
                last.start()
        out_ref[...] = acc[0, aligned(core * rows, rows, rows), own_at]
        last.wait_send()

    @pl.when(jnp.logical_not(holder))
    def _():
        last.wait_recv()
        for copy in to_mate:
            copy.wait_send()

    @pl.when(end)
    def _():
        for copy in inward:
            copy.wait_send()

    @pl.when(jnp.logical_not(end))
    def _():
        for copy in across:
            copy.wait_send()

    for copy in (*gather, *spread, *shared, *given):
        copy.wait_send()


def direct(half, metric, survive):
    aux_local, occ_local, ao = half.shape
    n_aux, n_orb = lax.axis_size("aux"), lax.axis_size("orb")
    part = occ_local // n_aux
    blocks = gated(half, survive).transpose(1, 0, 2).reshape(n_aux, part * aux_local, ao)
    n_fit = n_aux * aux_local
    width = -(-n_fit // 128) * 128
    metric = jnp.pad(metric, ((0, 0), (0, width - n_fit)))
    parts = 3
    slab = n_fit * part // parts
    rows, panel = ao // n_orb, ao // n_aux
    dma = pltpu.SemaphoreType.DMA
    bf16, i16 = jnp.bfloat16, jnp.int16
    return pl.pallas_call(
        functools.partial(kernel, aux_local),
        out_shape=jax.ShapeDtypeStruct((rows, panel), F32),
        in_specs=[pl.BlockSpec(memory_space=pltpu.VMEM)] * 2,
        out_specs=pl.BlockSpec(memory_space=pltpu.VMEM),
        scratch_shapes=[
            pltpu.VMEM((4, parts, slab, ao), bf16),
            pltpu.VMEM((4 * slab, 3 * panel), bf16),
            pltpu.VMEM((2, panel, 4 * slab), bf16),
            pltpu.VMEM((2, panel, 2 * panel), F32),
            pltpu.VMEM((n_fit, width), bf16),
            pltpu.VMEM((slab, slab), bf16),
            pltpu.VMEM((4, rows + 16, panel), i16),
            pltpu.VMEM((4, rows + 16, panel), i16),
            pltpu.VMEM((4, rows + 16, panel), i16),
            pltpu.VMEM((6, rows + 16, panel), i16),
            dma((4,)), dma((4,)),
            dma((3 * parts,)), dma((n_aux * parts,)),
            dma((20 * parts,)), dma((32 * parts,)),
            dma((4,)), dma((4,)),
            dma((4,)), dma((6,)),
            dma((1,)), dma((1,)),
        ],
        compiler_params=pltpu.CompilerParams(
            collective_id=0, has_side_effects=True, vmem_limit_bytes=66 * 1000 * 1000
        ),
    )(blocks, metric)


def solution(mesh):
    square = mesh.shape["aux"] == 4 and mesh.shape["orb"] == 8
    return jax.shard_map(
        direct if square else plain,
        mesh=mesh,
        in_specs=(P("aux", "orb", None), P("aux", None), P("aux", "orb", None)),
        out_specs=P("orb", "aux"),
        check_vma=False,
    )
```

time: 269 us -> 195 us (0.72)
  Pallas kernels: 257 us -> 183 us
    pallas_call x1, Pallas kernels: 257 us -> 183 us  [direct(): pl.pallas_call(functools.partial(kernel, aux_local), out_shape=jax.ShapeD...]
where the time goes in v2:
time: 195 us
  Pallas kernels  183 us (94%)
  local copies, waits for them, and re-layouts  7.82 us (4%)
  other arithmetic  3.48 us (2%)
    pallas_call x1, Pallas kernels, direct(): pl.pallas_call(functools.partial(kernel, aux_local), out_shape=jax.ShapeD...  183 us
    transpose x1, local copies, waits for them, and re-layouts, direct(): gated(half, survive).transpose(1, 0, 2).reshape(n_aux, part * aux_local, ao)  4.7 us

profile of v2, /device:TPU:0, one launch (start us, length us, event | category | flops | bytes accessed | tf_op | source)
XLA Modules:
  0.0 194.6 jit_solution(4543653716013607539)
XLA Ops:
  0.0 0.7 convert_bitcast_fusion
  0.7 0.1 mul.18
  0.8 2.8 %multiply_bitcast_fusion = bf16[48,16,3072]{2,0,1:T(8,128)(2,1)S(1)} fusion(bf16[16,48,3072]{2,1,0:T(8,128)(2,1)} %param.3, bf16[48,3072]{1,0:T(8,128)(2,1)S(1)} %bitcast.11), kind=kLoop, calls=%fused_computation | loop fusion | flops 2359296 | bytes 9732096 | tf_op jit(solution)/shard_map/transpose | solution.py:361
  3.7 0.0 copy-start
  3.7 4.7 %copy.4 = bf16[48,16,3072]{2,1,0:T(8,128)(2,1)} copy(bf16[48,16,3072]{2,0,1:T(8,128)(2,1)S(1)} %multiply_bitcast_fusion) | data formatting | bytes 9437184 | tf_op jit(solution)/shard_map/transpose | solution.py:361
  8.4 0.0 copy-done
  8.4 0.6 pad.4.metric_ref
  9.0 183.3 %shard_map.37 = f32[384,768]{1,0:T(8,128)} custom-call(bf16[4,192,3072]{2,1,0:T(8,128)(2,1)} %bitcast.10, bf16[16,128]{1,0:T(8,128)(2,1)} %pad.4.metric_ref), custom_call_target="tpu_custom_call" | custom-call | tf_op jit(solution)/shard_map/pallas_call | solution.py:370
  192.2 2.4 %copy.9 = f32[384,768]{1,0:T(8,128)} copy(f32[384,768]{1,0:T(8,128)} %shard_map.37) | data formatting | bytes 2359296
  (1 shorter events, 0.0 us)
Async XLA Ops:
  3.7 4.7 %copy-start = (bf16[16,64]{1,0:T(8,128)(2,1)S(1)}, bf16[16,64]{1,0:T(8,128)(2,1)}, u32[]{:S(2)}) copy-start(bf16[16,64]{1,0:T(8,128)(2,1)} %param.4) | copy-start | bytes 6148

commit v3 on v2

v3 whole, which is shorter than its diff:
```python
import functools

import jax
import jax.numpy as jnp
from jax import lax
from jax.experimental import pallas as pl
from jax.experimental.pallas import tpu as pltpu
from jax.sharding import PartitionSpec as P

MESH = pl.DeviceIdType.MESH
F32 = jnp.float32


def gated(half, survive):
    aux_local, occ_local, ao_count = half.shape
    blocks_aux, blocks_occ, blocks_ao = survive.shape
    gate = survive.astype(jnp.bfloat16)
    shaped = half.reshape(
        blocks_aux, aux_local, blocks_occ, occ_local // blocks_occ, blocks_ao, ao_count // blocks_ao
    )
    return (shaped * gate[:, None, :, None, :, None]).reshape(aux_local, occ_local, ao_count)


def plain(half, metric, survive):
    aux_local, occ_local, ao_count = half.shape
    portion = lax.all_gather(gated(half, survive), "aux", axis=0, tiled=True)
    fit_total = jnp.dot(metric, portion.reshape(portion.shape[0], -1), preferred_element_type=F32)
    fitted = fit_total.astype(jnp.bfloat16).reshape(aux_local, occ_local, ao_count)
    group_width = ao_count // lax.axis_size("orb")
    row_start = lax.axis_index("orb") * group_width
    flat_rows = lax.all_gather(fitted, "orb", axis=1, tiled=True).reshape(-1, ao_count)
    left_rows = lax.dynamic_slice_in_dim(flat_rows, row_start, group_width, 1)
    partial_k = lax.dot_general(
        left_rows, flat_rows, (((0,), (0,)), ((), ())), preferred_element_type=F32
    )
    return lax.psum_scatter(partial_k, "aux", scatter_dimension=1, tiled=True)

TOP = 32000.0
FINE = 256.0


def kernel(
    aux_local, sizes, m_ref, metric_ref, out_ref, held, fit, left, early, acc, whole, kron_four, kron_two,
    rs_out, rs_in, z_in,
    gs, gr, zs, zr, fs, fr, rs, rr, cs, cr, ws, wr,
):
    z = lax.axis_index("aux")
    orb = lax.axis_index("orb")
    n_aux = m_ref.shape[0]
    parts = len(sizes)
    begins = [sum(sizes[:q]) for q in range(parts)]
    panel = acc.shape[1]
    pieces = 4
    rows = panel // pieces
    chip = orb // 2
    core = orb % 2
    x, y = chip % 2, chip // 2
    x_chip = chip + 1 - 2 * x
    y_chip = chip + 2 - 4 * y
    partner = orb + 1 - 2 * core
    other_chip = core * x_chip + (1 - core) * y_chip
    rs_peer = 2 * other_chip + core
    unused = core * (3 - 3 * y) + (1 - core) * (1 + x)
    odd_panel = 6 - unused - 3
    side = z // 2
    end = z % 3 == 0
    mate = z + 1 - 2 * (z % 2)
    far_end = 3 - 3 * side
    far_inner = 2 - side
    near_block = core * (1 + side) + (1 - core) * 3 * side
    far_block = 3 - near_block
    holder = near_block == z

    barrier = pltpu.get_barrier_semaphore()
    for d in (1, 2, 3):
        pl.semaphore_signal(
            barrier, inc=1, device_id={"aux": (z + d) % n_aux, "orb": orb}, device_id_type=MESH
        )
    for o in (partner, 2 * x_chip, 2 * x_chip + 1, 2 * y_chip, 2 * y_chip + 1):
        pl.semaphore_signal(barrier, inc=1, device_id={"aux": z, "orb": o}, device_id_type=MESH)
    pl.semaphore_wait(barrier, 8)

    def remote(src, dst, send, recv, a, o):
        return pltpu.make_async_remote_copy(
            src_ref=src, dst_ref=dst, send_sem=send, recv_sem=recv,
            device_id={"aux": a, "orb": o}, device_id_type=MESH,
        )

    def aligned(start, size, unit_of=128):
        return pl.ds(pl.multiple_of(start, unit_of), size)

    metric_rows = aligned(z * aux_local, aux_local, aux_local)
    gather = []
    for d in (1, 3, 2):
        copy = remote(metric_ref, whole.at[metric_rows], gs.at[d], gr.at[d], (z + d) % n_aux, orb)
        copy.start()
        gather.append(copy)

    def given_rows(q):
        return pl.ds(begins[q] * aux_local, sizes[q] * aux_local)

    def held_rows(source, q):
        unit = sizes[q] * aux_local
        return aligned(begins[q] * aux_local * n_aux + source * unit, unit, unit)

    MATE, FAR_END, FAR_INNER = 1, 2, 3
    sources = (z, mate, far_end, far_inner)

    def spread(r, q):
        there = sources[r]
        return remote(
            m_ref.at[there, given_rows(q)], held.at[0, held_rows(z, q)],
            zs.at[r * parts + q], zr.at[z * parts + q], there, orb,
        )

    @pl.when(end)
    def _():
        for r, q in (
            (FAR_END, 0), (FAR_END, 1), (FAR_END, 2), (FAR_END, 3), (MATE, 0), (FAR_INNER, 0),
            (MATE, 1), (FAR_INNER, 1), (MATE, 2), (MATE, 3), (FAR_INNER, 2), (FAR_INNER, 3),
        ):
            spread(r, q).start()

    @pl.when(jnp.logical_not(end))
    def _():
        for r, q in (
            (FAR_END, 0), (MATE, 0), (FAR_INNER, 0), (MATE, 1), (FAR_END, 1), (MATE, 2),
            (FAR_INNER, 1), (MATE, 3), (FAR_END, 2), (FAR_END, 3), (FAR_INNER, 2), (FAR_INNER, 3),
        ):
            spread(r, q).start()

    def recv_at(slot, r, q, k):
        return fr.at[((slot * 4 + r) * parts + q) * 2 + k]

    def shares(r, q):
        source = sources[r]
        at = held_rows(source, q)

        def cut(columns):
            if r == 0:
                return m_ref.at[z, given_rows(q), columns]
            return held.at[0, at, columns]

        jobs = [(partner, 1, pl.ds(0, 4 * panel), 0)]
        for o, slot, first, pair in (
            (2 * x_chip, 2 + core, 3 - 3 * x, 2 * x),
            (2 * y_chip + 1, 2 + core, 1 - y, 2 - y),
        ):
            jobs += [
                (o, slot, aligned(first * panel, panel), 0),
                (o, slot, aligned(pair * panel, 2 * panel), 1),
            ]
        return [
            remote(
                cut(columns), held.at[slot, at, columns],
                fs.at[(n * 4 + r) * parts + q], recv_at(slot, r, q, k), z, o,
            )
            for n, (o, slot, columns, k) in enumerate(jobs)
        ]

    def share(r, q):
        for copy in shares(r, q):
            copy.start()

    def arrive(r, q):
        here = held.at[0, held_rows(sources[r], q)]
        remote(here, here, zs.at[q], zr.at[sources[r] * parts + q], mate, orb).wait_recv()
        share(r, q)

    for q in range(parts):
        share(0, q)

    def slots_of(q):
        first = core * y + (1 - core) * 3 * x
        pair = core * (1 + y) + (1 - core) * 2 * (1 - x)
        one, two = aligned(first * panel, panel), aligned(pair * panel, 2 * panel)
        for r in range(4):
            at = held_rows(sources[r], q)
            for slot, k, columns in (
                (1, 0, pl.ds(0, 4 * panel)), (2, 0, one), (2, 1, two), (3, 0, one), (3, 1, two)
            ):
                here = held.at[slot, at, columns]
                remote(here, here, fs.at[0], recv_at(slot, r, q, k), z, partner).wait_recv()

    def build_kron(kron_ref):
        depth, wide = kron_ref.shape[0], whole.shape[1]
        unit = depth // n_aux

        def aux_of(r):
            return lax.div(r, unit) * aux_local + lax.rem(r, aux_local)

        def orbital_of(r):
            return lax.div(lax.rem(r, unit), aux_local)

        i32, bf16 = jnp.int32, kron_ref.dtype
        by_row = aux_of(lax.broadcasted_iota(i32, (wide, depth), 1))
        pick = jnp.where(by_row == lax.broadcasted_iota(i32, (wide, depth), 0), 1.0, 0.0)
        spread_cols = jnp.dot(whole[...], pick.astype(bf16), preferred_element_type=F32).astype(bf16)
        by_col = aux_of(lax.broadcasted_iota(i32, (depth, whole.shape[0]), 0))
        take = jnp.where(by_col == lax.broadcasted_iota(i32, (depth, whole.shape[0]), 1), 1.0, 0.0)
        both = jnp.dot(take.astype(bf16), spread_cols, preferred_element_type=F32)
        same = orbital_of(lax.broadcasted_iota(i32, (depth, depth), 0)) == orbital_of(
            lax.broadcasted_iota(i32, (depth, depth), 1)
        )
        kron_ref[...] = jnp.where(same, both, 0.0).astype(bf16)

    def place(p):
        return jnp.where(p == core, 0, jnp.where(p == 3 - core, 1, 2))

    def depth_of(q):
        return 4 * sizes[q] * aux_local * n_aux

    fit_at = (0, 0, 0, depth_of(2))

    def fit_part(q):
        slab = sizes[q] * aux_local * n_aux
        kron_ref = kron_four if sizes[q] == sizes[0] else kron_two
        base = begins[q] * aux_local * n_aux

        @pl.loop(0, 4)
        def _(slot):
            for n, p in enumerate((core, 3 - core, odd_panel)):
                fit[aligned(fit_at[q] + slot * slab, slab, slab), pl.ds(n * panel, panel)] = jnp.dot(
                    kron_ref[...], held[slot, pl.ds(base, slab), aligned(p * panel, panel)],
                    preferred_element_type=F32,
                ).astype(fit.dtype)

    def turn(p, q):
        chosen = other_chip if p else chip
        fitted = fit[pl.ds(fit_at[q], depth_of(q)), aligned(place(chosen) * panel, panel)]
        if p:
            early[:, pl.ds(0, depth_of(q))] = fitted.T
        else:
            left[:, pl.ds(fit_at[q], depth_of(q))] = fitted.T

    step = 2 * panel // 3
    far_tiles = ((1 - side) * step, (2 - side) * step)
    near_tile = side * 2 * step

    def contract(p, tile, q, begin):
        at = aligned(tile, step)
        if q is None:
            deep = fit_at[-1] + depth_of(parts - 1)
            more = jnp.dot(left[...], fit[pl.ds(0, deep), at], preferred_element_type=F32)
        elif p:
            more = jnp.dot(
                early[:, pl.ds(0, depth_of(q))], fit[pl.ds(fit_at[q], depth_of(q)), at],
                preferred_element_type=F32,
            )
        else:
            more = jnp.dot(
                left[:, pl.ds(fit_at[q], depth_of(q))], fit[pl.ds(fit_at[q], depth_of(q)), at],
                preferred_element_type=F32,
            )
        acc[p, :, at] = more if begin else acc[p, :, at] + more

    def contract_all(p, q, begin):
        @pl.loop(0, 3)
        def _(t):
            contract(p, t * step, q, begin)

    near, far = side, 1 - side
    strip = 32
    half = pieces // 2
    order = [(1 - core) * half + i for i in range(half)] + [core * half + i for i in range(half)]

    def block_at(block):
        return aligned(block * panel, panel)

    def quantize(p, block, h, target):
        at = block_at(block)

        def tops(t, top):
            some = acc[p, aligned(h * rows + t * strip, strip, strip), at]
            return jnp.maximum(top, jnp.max(jnp.abs(some).reshape(strip // 8, 8, panel), axis=0))

        top = lax.fori_loop(0, rows // strip, tops, jnp.zeros((8, panel), F32))
        top = jnp.maximum(jnp.max(top, axis=0, keepdims=True), 1e-30)
        level = jnp.ceil(jnp.log2(top) * FINE)
        scale = TOP * jnp.exp2(level * (-1.0 / FINE))

        @pl.loop(0, rows // strip)
        def _(t):
            some = acc[p, aligned(h * rows + t * strip, strip, strip), at]
            target[aligned(t * strip, strip, strip), :] = (
                jnp.round(some * scale).astype(jnp.int32).astype(jnp.int16)
            )

        target[pl.ds(rows, 16), :] = jnp.broadcast_to(
            level.astype(jnp.int32), (16, panel)
        ).astype(jnp.int16)

    def add_in(source, block, h):
        at = block_at(block)
        level = source[pl.ds(rows, 16), :].astype(F32)[:1]
        scale = jnp.exp2(level * (1.0 / FINE)) * (1.0 / TOP)

        @pl.loop(0, rows // strip)
        def _(t):
            here = aligned(h * rows + t * strip, strip, strip)
            some = source[aligned(t * strip, strip, strip), :].astype(F32)
            acc[0, here, at] = acc[0, here, at] + some * scale

    for q in range(parts):
        held[0, held_rows(z, q), :] = m_ref[z, given_rows(q), :]
    whole[metric_rows, :] = metric_ref[...]

    @pl.when(end)
    def _():
        for r, q in (
            (FAR_END, 0), (FAR_END, 1), (FAR_END, 2), (FAR_END, 3), (FAR_INNER, 0), (MATE, 0), (MATE, 1)
        ):
            arrive(r, q)

    @pl.when(jnp.logical_not(end))
    def _():
        for r, q in ((MATE, 0), (FAR_END, 0), (FAR_INNER, 0), (MATE, 1), (FAR_END, 1)):
            arrive(r, q)

    for copy in gather:
        copy.wait_recv()
    build_kron(kron_four)
    build_kron(kron_two)
    slots_of(0)
    fit_part(0)
    turn(0, 0)
    turn(1, 0)
    contract_all(1, 0, True)
    arrive(MATE, 2)
    contract_all(0, 0, True)
    arrive(MATE, 3)

    @pl.when(jnp.logical_not(end))
    def _():
        arrive(FAR_END, 2)
        arrive(FAR_END, 3)

    arrive(FAR_INNER, 1)
    slots_of(1)
    fit_part(1)
    turn(1, 1)
    turn(0, 1)
    contract_all(1, 1, False)
    arrive(FAR_INNER, 2)
    contract_all(0, 1, False)
    arrive(FAR_INNER, 3)
    slots_of(2)
    fit_part(2)
    turn(1, 2)
    contract_all(1, 2, False)
    slots_of(3)
    fit_part(3)
    turn(1, 3)

    def given(n):
        return remote(rs_out.at[n], rs_in.at[n], rs.at[n], rr.at[n], z, rs_peer)

    def give(block, n):
        quantize(1, block, order[n % pieces], rs_out.at[n])
        given(n).start()

    for tile in far_tiles:
        contract(1, tile, 3, False)
    give(far, 0)
    contract(1, near_tile, 3, False)
    give(near, pieces)
    for i in range(1, pieces):
        give(far, i)
        give(near, pieces + i)
    for q in range(2, parts):
        turn(0, q)
    for tile in (*far_tiles, near_tile):
        contract(0, tile, None, False)

    def along(n, into, there):
        return remote(rs_out.at[n], z_in.at[into], cs.at[n], cr.at[into], there, orb)

    inward = [along(i, i, mate) for i in range(pieces)]
    to_mate = [along(pieces + i, pieces + i, mate) for i in range(pieces)]
    across = [along(i, 2 * pieces + i, far_block) for i in range(pieces)]

    def pass_near(i):
        quantize(0, near, order[i], rs_out.at[pieces + i])
        to_mate[i].start()

    for i, h in enumerate(order):
        given(i).wait()
        add_in(rs_in.at[i], far, h)

        @pl.when(end)
        def _():
            quantize(0, far, h, rs_out.at[i])
            inward[i].start()

        @pl.when(jnp.logical_not(end))
        def _():
            inward[i].wait_recv()
            add_in(z_in.at[i], far, h)
            quantize(0, far, h, rs_out.at[i])
            across[i].start()

        given(pieces + i).wait()
        add_in(rs_in.at[pieces + i], near, h)

        @pl.when(jnp.logical_not(jnp.logical_or(holder, end)))
        def _():
            pass_near(i)

    @pl.when(jnp.logical_and(jnp.logical_not(holder), end))
    def _():
        for i in range(pieces):
            pass_near(i)

    own_at = block_at(near)

    def last(i):
        return remote(
            acc.at[0, aligned(order[i] * rows, rows, rows), own_at],
            out_ref.at[pl.ds(i * rows, rows)], ws.at[i], wr.at[i], z, partner,
        )

    @pl.when(holder)
    def _():
        for i, h in enumerate(order):
            to_mate[i].wait_recv()
            add_in(z_in.at[pieces + i], near, h)
        for i, h in enumerate(order):
            across[i].wait_recv()
            add_in(z_in.at[2 * pieces + i], near, h)
            if i < half:
                last(i).start()
            else:
                out_ref[pl.ds((i - half) * rows, rows), :] = acc[0, aligned(h * rows, rows, rows), own_at]
        for i in range(half):
            last(i).wait_send()

    @pl.when(jnp.logical_not(holder))
    def _():
        for i in range(half):
            last(i).wait_recv()
        for copy in to_mate:
            copy.wait_send()

    @pl.when(end)
    def _():
        for copy in inward:
            copy.wait_send()

    @pl.when(jnp.logical_not(end))
    def _():
        for copy in across:
            copy.wait_send()

    for copy in gather:
        copy.wait_send()
    for r in range(4):
        for q in range(parts):
            if r:
                spread(r, q).wait_send()
            for copy in shares(r, q):
                copy.wait_send()


def direct(half, metric, survive):
    aux_local, occ_local, ao = half.shape
    n_aux, n_orb = lax.axis_size("aux"), lax.axis_size("orb")
    part = occ_local // n_aux
    blocks = gated(half, survive).transpose(1, 0, 2).reshape(n_aux, part * aux_local, ao)
    n_fit = n_aux * aux_local
    width = -(-n_fit // 128) * 128
    metric = jnp.pad(metric, ((0, 0), (0, width - n_fit)))
    sizes = (part // 3, part // 3, part // 6, part // 6)
    parts = len(sizes)
    four, two = sizes[0] * n_fit, sizes[2] * n_fit
    late = 4 * four
    rows, panel = ao // n_orb, ao // n_aux
    dma = pltpu.SemaphoreType.DMA
    bf16, i16 = jnp.bfloat16, jnp.int16
    piece = (panel // 4 + 16, panel)
    return pl.pallas_call(
        functools.partial(kernel, aux_local, sizes),
        out_shape=jax.ShapeDtypeStruct((rows, panel), F32),
        in_specs=[pl.BlockSpec(memory_space=pltpu.VMEM)] * 2,
        out_specs=pl.BlockSpec(memory_space=pltpu.VMEM),
        scratch_shapes=[
            pltpu.VMEM((4, part * n_fit, ao), bf16),
            pltpu.VMEM((late, 3 * panel), bf16),
            pltpu.VMEM((panel, late), bf16),
            pltpu.VMEM((panel, 4 * four), bf16),
            pltpu.VMEM((2, panel, 2 * panel), F32),
            pltpu.VMEM((n_fit, width), bf16),
            pltpu.VMEM((four, four), bf16),
            pltpu.VMEM((two, two), bf16),
            pltpu.VMEM((8, *piece), i16),
            pltpu.VMEM((8, *piece), i16),
            pltpu.VMEM((12, *piece), i16),
            dma((4,)), dma((4,)),
            dma((4 * parts,)), dma((n_aux * parts,)),
            dma((20 * parts,)), dma((32 * parts,)),
            dma((8,)), dma((8,)),
            dma((8,)), dma((12,)),
            dma((2,)), dma((2,)),
        ],
        compiler_params=pltpu.CompilerParams(
            collective_id=0, has_side_effects=True, vmem_limit_bytes=66 * 1000 * 1000
        ),
    )(blocks, metric)


def solution(mesh):
    square = mesh.shape["aux"] == 4 and mesh.shape["orb"] == 8
    return jax.shard_map(
        direct if square else plain,
        mesh=mesh,
        in_specs=(P("aux", "orb", None), P("aux", None), P("aux", "orb", None)),
        out_specs=P("orb", "aux"),
        check_vma=False,
    )
```

time: 195 us -> 175 us (0.90)
  Pallas kernels: 183 us -> 164 us
    pallas_call x1, Pallas kernels: 183 us -> 164 us  [direct(): pl.pallas_call(functools.partial(kernel, aux_local, sizes), out_shape=jax...]
where the time goes in v3:
time: 175 us
  Pallas kernels  164 us (94%)
  local copies, waits for them, and re-layouts  7.82 us (4%)
  other arithmetic  3.48 us (2%)
    pallas_call x1, Pallas kernels, direct(): pl.pallas_call(functools.partial(kernel, aux_local, sizes), out_shape=jax...  164 us
    transpose x1, local copies, waits for them, and re-layouts, direct(): gated(half, survive).transpose(1, 0, 2).reshape(n_aux, part * aux_local, ao)  4.7 us

profile of v3, /device:TPU:0, one launch (start us, length us, event | category | flops | bytes accessed | tf_op | source)
XLA Modules:
  0.0 175.2 jit_solution(3874175031568810538)
XLA Ops:
  0.0 0.7 convert_bitcast_fusion
  0.7 0.1 mul.18
  0.8 2.8 %multiply_bitcast_fusion = bf16[48,16,3072]{2,0,1:T(8,128)(2,1)S(1)} fusion(bf16[16,48,3072]{2,1,0:T(8,128)(2,1)} %param.3, bf16[48,3072]{1,0:T(8,128)(2,1)S(1)} %bitcast.11), kind=kLoop, calls=%fused_computation | loop fusion | flops 2359296 | bytes 9732096 | tf_op jit(solution)/shard_map/transpose | solution.py:468
  3.7 0.0 copy-start
  3.7 4.7 %copy.4 = bf16[48,16,3072]{2,1,0:T(8,128)(2,1)} copy(bf16[48,16,3072]{2,0,1:T(8,128)(2,1)S(1)} %multiply_bitcast_fusion) | data formatting | bytes 9437184 | tf_op jit(solution)/shard_map/transpose | solution.py:468
  8.4 0.0 copy-done
  8.4 0.6 pad.4.metric_ref
  9.0 163.8 %shard_map.37 = f32[384,768]{1,0:T(8,128)} custom-call(bf16[4,192,3072]{2,1,0:T(8,128)(2,1)} %bitcast.10, bf16[16,128]{1,0:T(8,128)(2,1)} %pad.4.metric_ref), custom_call_target="tpu_custom_call" | custom-call | tf_op jit(solution)/shard_map/pallas_call | solution.py:480
  172.8 2.4 %copy.9 = f32[384,768]{1,0:T(8,128)} copy(f32[384,768]{1,0:T(8,128)} %shard_map.37) | data formatting | bytes 2359296
  (1 shorter events, 0.0 us)
Async XLA Ops:
  3.7 4.7 %copy-start = (bf16[16,64]{1,0:T(8,128)(2,1)S(1)}, bf16[16,64]{1,0:T(8,128)(2,1)}, u32[]{:S(2)}) copy-start(bf16[16,64]{1,0:T(8,128)(2,1)} %param.4) | copy-start | bytes 6148

commit v4 on v3

--- a/solution.py
+++ b/solution.py
@@ -40,18 +40,22 @@
 
 
 def kernel(
-    aux_local, sizes, m_ref, metric_ref, out_ref, held, fit, left, early, acc, whole, kron_four, kron_two,
+    sizes, half_ref, metric_ref, survive_ref, out_ref, raw, m_ref, pick_ref, gate, metric_pad, held, fit, left, early, acc, whole, kron_four, kron_two,
     rs_out, rs_in, z_in,
-    gs, gr, zs, zr, fs, fr, rs, rr, cs, cr, ws, wr,
+    ls, gs, gr, zs, zr, fs, fr, rs, rr, cs, cr, ws, wr,
 ):
     z = lax.axis_index("aux")
     orb = lax.axis_index("orb")
     n_aux = m_ref.shape[0]
+    aux_local, occ_local, ao = raw.shape
     parts = len(sizes)
     begins = [sum(sizes[:q]) for q in range(parts)]
     panel = acc.shape[1]
-    pieces = 4
-    rows = panel // pieces
+    unit_rows = panel // 8
+    counts = [n * unit_rows for n in (1, 1, 2, 2, 1, 1)]
+    starts = [n * unit_rows for n in (0, 1, 2, 0, 2, 3)]
+    offsets = [n * unit_rows for n in (0, 1, 2, 4, 6, 7)]
+    pieces = len(counts)
     chip = orb // 2
     core = orb % 2
     x, y = chip % 2, chip // 2
@@ -78,6 +82,30 @@
         )
     for o in (partner, 2 * x_chip, 2 * x_chip + 1, 2 * y_chip, 2 * y_chip + 1):
         pl.semaphore_signal(barrier, inc=1, device_id={"aux": z, "orb": o}, device_id_type=MESH)
+
+    tiles = ls.shape[0]
+    tile_width = ao // tiles
+    loads = []
+    for t in range(tiles):
+        at = pl.ds(t * tile_width, tile_width)
+        load = pltpu.make_async_copy(half_ref.at[:, :, at], raw.at[:, :, at], ls.at[t])
+        load.start()
+        loads.append(load)
+
+    count = aux_local * occ_local
+    out_row = lax.broadcasted_iota(jnp.int32, (count, count), 0)
+    in_row = lax.broadcasted_iota(jnp.int32, (count, count), 1)
+    wanted = lax.rem(out_row, aux_local) * occ_local + lax.div(out_row, aux_local)
+    pick_ref[...] = jnp.where(in_row == wanted, 1.0, 0.0).astype(pick_ref.dtype)
+    survived = survive_ref[...].astype(F32)
+    ao_blocks = survive_ref.shape[1]
+    block_width = ao // ao_blocks
+    for b in range(ao_blocks):
+        gate[:, pl.ds(b * block_width, block_width)] = jnp.broadcast_to(
+            survived[:, b : b + 1], (gate.shape[0], block_width)
+        )
+    metric_pad[...] = jnp.zeros_like(metric_pad)
+    metric_pad[:, pl.ds(0, metric_ref.shape[1])] = metric_ref[...]
     pl.semaphore_wait(barrier, 8)
 
     def remote(src, dst, send, recv, a, o):
@@ -92,7 +120,7 @@
     metric_rows = aligned(z * aux_local, aux_local, aux_local)
     gather = []
     for d in (1, 3, 2):
-        copy = remote(metric_ref, whole.at[metric_rows], gs.at[d], gr.at[d], (z + d) % n_aux, orb)
+        copy = remote(metric_pad, whole.at[metric_rows], gs.at[d], gr.at[d], (z + d) % n_aux, orb)
         copy.start()
         gather.append(copy)
 
@@ -113,24 +141,54 @@
             zs.at[r * parts + q], zr.at[z * parts + q], there, orb,
         )
 
+    def sort_rows(pair, first):
+        span = count // 2
+        rows_at = pl.multiple_of(pair * span, span)
+        for t in range(tiles):
+            at = pl.ds(t * tile_width, tile_width)
+            if first:
+                loads[t].wait()
+            sorted_rows = jnp.dot(
+                pick_ref[pl.ds(rows_at, span), :], raw[:, :, at].reshape(count, tile_width),
+                preferred_element_type=F32,
+            )
+            gated_rows = sorted_rows * gate[pl.ds(pair, 1), at]
+            m_ref[pl.ds(2 * pair, 2), :, at] = gated_rows.astype(m_ref.dtype).reshape(
+                2, span // 2, tile_width
+            )
+
+    sort_rows(1 - side, True)
+
     @pl.when(end)
     def _():
+        for q in range(parts):
+            spread(FAR_END, q).start()
+
+    @pl.when(jnp.logical_not(end))
+    def _():
         for r, q in (
-            (FAR_END, 0), (FAR_END, 1), (FAR_END, 2), (FAR_END, 3), (MATE, 0), (FAR_INNER, 0),
-            (MATE, 1), (FAR_INNER, 1), (MATE, 2), (MATE, 3), (FAR_INNER, 2), (FAR_INNER, 3),
+            (FAR_END, 0), (FAR_END, 1), (FAR_INNER, 0), (FAR_END, 2), (FAR_END, 3),
+            (FAR_END, 4), (FAR_INNER, 1), (FAR_INNER, 2), (FAR_INNER, 3), (FAR_INNER, 4),
         ):
             spread(r, q).start()
 
-    @pl.when(jnp.logical_not(end))
+    sort_rows(side, False)
+
+    @pl.when(end)
     def _():
         for r, q in (
-            (FAR_END, 0), (MATE, 0), (FAR_INNER, 0), (MATE, 1), (FAR_END, 1), (MATE, 2),
-            (FAR_INNER, 1), (MATE, 3), (FAR_END, 2), (FAR_END, 3), (FAR_INNER, 2), (FAR_INNER, 3),
+            (MATE, 0), (MATE, 1), (FAR_INNER, 0), (FAR_INNER, 1), (MATE, 2),
+            (MATE, 3), (MATE, 4), (FAR_INNER, 2), (FAR_INNER, 3), (FAR_INNER, 4),
         ):
             spread(r, q).start()
 
+    @pl.when(jnp.logical_not(end))
+    def _():
+        for q in range(parts):
+            spread(MATE, q).start()
+
     def recv_at(slot, r, q, k):
-        return fr.at[((slot * 4 + r) * parts + q) * 2 + k]
+        return fr.at[(((slot - 1) * 4 + r) * parts + q) * 2 + k]
 
     def shares(r, q):
         source = sources[r]
@@ -210,7 +268,7 @@
     def depth_of(q):
         return 4 * sizes[q] * aux_local * n_aux
 
-    fit_at = (0, 0, 0, depth_of(2))
+    fit_at = (0, 0, 0, depth_of(2), 2 * depth_of(2))
 
     def fit_part(q):
         slab = sizes[q] * aux_local * n_aux
@@ -234,8 +292,8 @@
             left[:, pl.ds(fit_at[q], depth_of(q))] = fitted.T
 
     step = 2 * panel // 3
-    far_tiles = ((1 - side) * step, (2 - side) * step)
-    near_tile = side * 2 * step
+    mixed = jnp.logical_not(jnp.logical_or(end, holder))
+    far_edge, near_edge = (1 - side) * 2 * step, side * 2 * step
 
     def contract(p, tile, q, begin):
         at = aligned(tile, step)
@@ -262,59 +320,78 @@
     near, far = side, 1 - side
     strip = 32
     half = pieces // 2
-    order = [(1 - core) * half + i for i in range(half)] + [core * half + i for i in range(half)]
+    sides_of = [1 - core] * half + [core] * half
+    order = [sides_of[i] * 4 * unit_rows + starts[i] for i in range(pieces)]
+    FAR, NEAR, MORE = 0, 1, 2
 
     def block_at(block):
         return aligned(block * panel, panel)
 
-    def quantize(p, block, h, target):
+    def tops_of(p, block):
         at = block_at(block)
 
         def tops(t, top):
-            some = acc[p, aligned(h * rows + t * strip, strip, strip), at]
+            some = acc[p, aligned(t * strip, strip, strip), at]
             return jnp.maximum(top, jnp.max(jnp.abs(some).reshape(strip // 8, 8, panel), axis=0))
 
-        top = lax.fori_loop(0, rows // strip, tops, jnp.zeros((8, panel), F32))
-        top = jnp.maximum(jnp.max(top, axis=0, keepdims=True), 1e-30)
-        level = jnp.ceil(jnp.log2(top) * FINE)
+        top = lax.fori_loop(0, panel // strip, tops, jnp.zeros((8, panel), F32))
+        return jnp.max(top, axis=0, keepdims=True)
+
+    def level_of(top):
+        return jnp.ceil(jnp.log2(jnp.maximum(top, 1e-30)) * FINE)
+
+    def rows_of(i):
+        if i == 0:
+            return pl.ds(0, 16 + counts[0])
+        return pl.ds(16 + offsets[i], counts[i])
+
+    def bound_of(source):
+        return jnp.exp2(source[pl.ds(0, 16), :].astype(F32)[:1] * (1.0 / FINE))
+
+    def quantize(p, block, i, level, target):
+        at = block_at(block)
         scale = TOP * jnp.exp2(level * (-1.0 / FINE))
 
-        @pl.loop(0, rows // strip)
+        @pl.loop(0, counts[i] // strip)
         def _(t):
-            some = acc[p, aligned(h * rows + t * strip, strip, strip), at]
-            target[aligned(t * strip, strip, strip), :] = (
+            some = acc[p, aligned(order[i] + t * strip, strip, strip), at]
+            target[aligned(16 + offsets[i] + t * strip, strip, 16), :] = (
                 jnp.round(some * scale).astype(jnp.int32).astype(jnp.int16)
             )
 
-        target[pl.ds(rows, 16), :] = jnp.broadcast_to(
-            level.astype(jnp.int32), (16, panel)
-        ).astype(jnp.int16)
-
-    def add_in(source, block, h):
+        if i == 0:
+            target[pl.ds(0, 16), :] = jnp.broadcast_to(
+                level.astype(jnp.int32), (16, panel)
+            ).astype(jnp.int16)
+
+    def add_in(source, bound, block, i):
         at = block_at(block)
-        level = source[pl.ds(rows, 16), :].astype(F32)[:1]
-        scale = jnp.exp2(level * (1.0 / FINE)) * (1.0 / TOP)
-
-        @pl.loop(0, rows // strip)
+        scale = bound * (1.0 / TOP)
+
+        @pl.loop(0, counts[i] // strip)
         def _(t):
-            here = aligned(h * rows + t * strip, strip, strip)
-            some = source[aligned(t * strip, strip, strip), :].astype(F32)
+            here = aligned(order[i] + t * strip, strip, strip)
+            some = source[aligned(16 + offsets[i] + t * strip, strip, 16), :].astype(F32)
             acc[0, here, at] = acc[0, here, at] + some * scale
 
     for q in range(parts):
         held[0, held_rows(z, q), :] = m_ref[z, given_rows(q), :]
-    whole[metric_rows, :] = metric_ref[...]
+    whole[metric_rows, :] = metric_pad[...]
 
     @pl.when(end)
     def _():
         for r, q in (
-            (FAR_END, 0), (FAR_END, 1), (FAR_END, 2), (FAR_END, 3), (FAR_INNER, 0), (MATE, 0), (MATE, 1)
+            (FAR_END, 0), (FAR_END, 1), (FAR_END, 2), (FAR_END, 3), (FAR_END, 4),
+            (FAR_INNER, 0), (FAR_INNER, 1), (MATE, 0), (MATE, 1),
         ):
             arrive(r, q)
 
     @pl.when(jnp.logical_not(end))
     def _():
-        for r, q in ((MATE, 0), (FAR_END, 0), (FAR_INNER, 0), (MATE, 1), (FAR_END, 1)):
+        for r, q in (
+            (MATE, 0), (MATE, 1), (FAR_END, 0), (FAR_END, 1), (MATE, 2), (FAR_INNER, 0),
+            (MATE, 3), (MATE, 4),
+        ):
             arrive(r, q)
 
     for copy in gather:
@@ -326,130 +403,194 @@
     turn(0, 0)
     turn(1, 0)
     contract_all(1, 0, True)
-    arrive(MATE, 2)
     contract_all(0, 0, True)
-    arrive(MATE, 3)
+
+    @pl.when(end)
+    def _():
+        for q in (2, 3, 4):
+            arrive(MATE, q)
 
     @pl.when(jnp.logical_not(end))
     def _():
-        arrive(FAR_END, 2)
-        arrive(FAR_END, 3)
-
-    arrive(FAR_INNER, 1)
+        for q in (2, 3, 4):
+            arrive(FAR_END, q)
+        arrive(FAR_INNER, 1)
+
+    arrive(FAR_INNER, 2)
     slots_of(1)
     fit_part(1)
     turn(1, 1)
     turn(0, 1)
     contract_all(1, 1, False)
-    arrive(FAR_INNER, 2)
+    arrive(FAR_INNER, 3)
     contract_all(0, 1, False)
-    arrive(FAR_INNER, 3)
     slots_of(2)
     fit_part(2)
     turn(1, 2)
+    arrive(FAR_INNER, 4)
     contract_all(1, 2, False)
     slots_of(3)
     fit_part(3)
     turn(1, 3)
-
-    def given(n):
-        return remote(rs_out.at[n], rs_in.at[n], rs.at[n], rr.at[n], z, rs_peer)
-
-    def give(block, n):
-        quantize(1, block, order[n % pieces], rs_out.at[n])
-        given(n).start()
-
-    for tile in far_tiles:
-        contract(1, tile, 3, False)
-    give(far, 0)
-    contract(1, near_tile, 3, False)
-    give(near, pieces)
-    for i in range(1, pieces):
-        give(far, i)
-        give(near, pieces + i)
+    contract_all(1, 3, False)
+    slots_of(4)
+    fit_part(4)
+    turn(1, 4)
+
+    def given(k, i):
+        at, n = rows_of(i), k * pieces + i
+        return remote(rs_out.at[k, at], rs_in.at[k, at], rs.at[n], rr.at[n], z, rs_peer)
+
+    def give(k, level, i):
+        quantize(1, (far, near)[k], i, level, rs_out.at[k])
+        given(k, i).start()
+
+    contract(1, far_edge, 4, False)
+    contract(1, step, 4, False)
+    far_level = level_of(tops_of(1, far))
+    F, N = FAR, NEAR
+    hold = jnp.logical_and(holder, jnp.logical_not(end))
+    in_order = tuple((k, i) for k in (F, N) for i in range(pieces))
+    mixed_order = (
+        (F, 0), (F, 1), (F, 2), (N, 0), (F, 3), (N, 1), (F, 4), (N, 2), (N, 3), (F, 5), (N, 4), (N, 5),
+    )
+    hold_order = (
+        (F, 0), (F, 1), (N, 0), (N, 1), (N, 2), (F, 2), (N, 3), (F, 3), (F, 4), (F, 5), (N, 4), (N, 5),
+    )
+    for i in range(2):
+        give(FAR, far_level, i)
+
+    @pl.when(mixed)
+    def _():
+        give(FAR, far_level, 2)
+
+    @pl.when(end)
+    def _():
+        for i in range(2, pieces):
+            give(FAR, far_level, i)
+
     for q in range(2, parts):
         turn(0, q)
-    for tile in (*far_tiles, near_tile):
-        contract(0, tile, None, False)
-
-    def along(n, into, there):
-        return remote(rs_out.at[n], z_in.at[into], cs.at[n], cr.at[into], there, orb)
-
-    inward = [along(i, i, mate) for i in range(pieces)]
-    to_mate = [along(pieces + i, pieces + i, mate) for i in range(pieces)]
-    across = [along(i, 2 * pieces + i, far_block) for i in range(pieces)]
-
-    def pass_near(i):
-        quantize(0, near, order[i], rs_out.at[pieces + i])
-        to_mate[i].start()
-
-    for i, h in enumerate(order):
-        given(i).wait()
-        add_in(rs_in.at[i], far, h)
-
-        @pl.when(end)
-        def _():
-            quantize(0, far, h, rs_out.at[i])
-            inward[i].start()
-
-        @pl.when(jnp.logical_not(end))
-        def _():
-            inward[i].wait_recv()
-            add_in(z_in.at[i], far, h)
-            quantize(0, far, h, rs_out.at[i])
-            across[i].start()
-
-        given(pieces + i).wait()
-        add_in(rs_in.at[pieces + i], near, h)
-
-        @pl.when(jnp.logical_not(jnp.logical_or(holder, end)))
-        def _():
-            pass_near(i)
-
-    @pl.when(jnp.logical_and(jnp.logical_not(holder), end))
-    def _():
-        for i in range(pieces):
-            pass_near(i)
+    contract(0, far_edge, None, False)
+    contract(0, step, None, False)
+    far_top = tops_of(0, far)
+
+    def along(k, i, into, there):
+        at, n = rows_of(i), k * pieces + i
+        return remote(
+            rs_out.at[k, at], z_in.at[into, at], cs.at[n], cr.at[into * pieces + i], there, orb
+        )
+
+    def inward(i):
+        return along(FAR, i, FAR, mate)
+
+    def to_mate(i):
+        return along(NEAR, i, NEAR, mate)
+
+    def across(i):
+        return along(FAR, i, MORE, far_inner)
+
+    def near_given(i):
+        given(NEAR, i).wait()
+        add_in(rs_in.at[NEAR], bound_of(rs_in.at[NEAR]), near, i)
+
+    def far_given(i):
+        given(FAR, i).wait()
+        add_in(rs_in.at[FAR], bound_of(rs_in.at[FAR]), far, i)
+
+    def far_to_mate(i):
+        far_given(i)
+        quantize(0, far, i, level_of(far_top + bound_of(rs_in.at[FAR])), rs_out.at[FAR])
+        inward(i).start()
+
+    def far_across(i):
+        far_given(i)
+        inward(i).wait_recv()
+        more = bound_of(z_in.at[FAR])
+        add_in(z_in.at[FAR], more, far, i)
+        total = far_top + bound_of(rs_in.at[FAR]) + more
+        quantize(0, far, i, level_of(total), rs_out.at[FAR])
+        across(i).start()
 
     own_at = block_at(near)
 
     def last(i):
         return remote(
-            acc.at[0, aligned(order[i] * rows, rows, rows), own_at],
-            out_ref.at[pl.ds(i * rows, rows)], ws.at[i], wr.at[i], z, partner,
+            acc.at[0, aligned(order[i], counts[i], counts[i]), own_at],
+            out_ref.at[pl.ds(starts[i], counts[i])], ws.at[i], wr.at[i], z, partner,
         )
 
-    @pl.when(holder)
-    def _():
-        for i, h in enumerate(order):
-            to_mate[i].wait_recv()
-            add_in(z_in.at[pieces + i], near, h)
-        for i, h in enumerate(order):
-            across[i].wait_recv()
-            add_in(z_in.at[2 * pieces + i], near, h)
-            if i < half:
-                last(i).start()
+    def settle(i):
+        return pltpu.make_async_copy(
+            acc.at[0, aligned(order[i], counts[i], counts[i]), own_at],
+            out_ref.at[pl.ds(starts[i], counts[i])], ws.at[i],
+        )
+
+    @pl.when(end)
+    def _():
+        far_to_mate(0)
+
+    @pl.when(jnp.logical_not(end))
+    def _():
+        far_across(0)
+
+    contract(1, near_edge, 4, False)
+    near_level = level_of(tops_of(1, near))
+    def give_rest(sequence):
+        for k, i in sequence:
+            give(k, (far_level, near_level)[k], i)
+
+    @pl.when(mixed)
+    def _():
+        give_rest(mixed_order[3:])
+
+    @pl.when(hold)
+    def _():
+        give_rest(hold_order[2:])
+
+    @pl.when(end)
+    def _():
+        give_rest(in_order[pieces:])
+
+    contract(0, near_edge, None, False)
+    near_top = tops_of(0, near)
+
+    def near_pass(i, combined):
+        near_given(i)
+        total = near_top + bound_of(rs_in.at[NEAR])
+        if combined:
+            across(i).wait_recv()
+            more = bound_of(z_in.at[MORE])
+            add_in(z_in.at[MORE], more, near, i)
+            total = total + more
+        quantize(0, near, i, level_of(total), rs_out.at[NEAR])
+        to_mate(i).start()
+
+    @pl.when(mixed)
+    def _():
+        for k, i in mixed_order[1:]:
+            if k == F:
+                far_across(i)
             else:
-                out_ref[pl.ds((i - half) * rows, rows), :] = acc[0, aligned(h * rows, rows, rows), own_at]
-        for i in range(half):
-            last(i).wait_send()
-
-    @pl.when(jnp.logical_not(holder))
-    def _():
-        for i in range(half):
-            last(i).wait_recv()
-        for copy in to_mate:
-            copy.wait_send()
+                near_pass(i, True)
 
     @pl.when(end)
     def _():
-        for copy in inward:
-            copy.wait_send()
-
-    @pl.when(jnp.logical_not(end))
-    def _():
-        for copy in across:
-            copy.wait_send()
+        for i in range(1, pieces):
+            far_to_mate(i)
+
+    @pl.when(hold)
+    def _():
+        for k, i in hold_order[1:]:
+            if k == F:
+                far_across(i)
+            else:
+                near_given(i)
+
+    @pl.when(jnp.logical_and(end, jnp.logical_not(holder)))
+    def _():
+        for i in range(pieces):
+            near_pass(i, False)
 
     for copy in gather:
         copy.wait_send()
@@ -460,29 +601,73 @@
             for copy in shares(r, q):
                 copy.wait_send()
 
+    def finish(crossed):
+        for i in range(pieces):
+            to_mate(i).wait_recv()
+            add_in(z_in.at[NEAR], bound_of(z_in.at[NEAR]), near, i)
+            if crossed:
+                across(i).wait_recv()
+                add_in(z_in.at[MORE], bound_of(z_in.at[MORE]), near, i)
+            if i < half:
+                last(i).start()
+            else:
+                settle(i).start()
+        for i in range(half):
+            last(i).wait_send()
+            settle(half + i).wait()
+
+    @pl.when(jnp.logical_and(holder, end))
+    def _():
+        for i in range(pieces):
+            near_given(i)
+        finish(False)
+
+    @pl.when(hold)
+    def _():
+        finish(True)
+
+    @pl.when(jnp.logical_not(holder))
+    def _():
+        for i in range(half):
+            last(i).wait_recv()
+
+    for i in range(pieces):
+        inward(i).wait_send()
+
+    @pl.when(jnp.logical_not(holder))
+    def _():
+        for i in range(pieces):
+            to_mate(i).wait_send()
+
 
 def direct(half, metric, survive):
     aux_local, occ_local, ao = half.shape
     n_aux, n_orb = lax.axis_size("aux"), lax.axis_size("orb")
     part = occ_local // n_aux
-    blocks = gated(half, survive).transpose(1, 0, 2).reshape(n_aux, part * aux_local, ao)
+    if survive.shape[:2] != (1, 2) or part % 6:
+        return plain(half, metric, survive)
+    survive = survive.reshape(survive.shape[1:])
     n_fit = n_aux * aux_local
     width = -(-n_fit // 128) * 128
-    metric = jnp.pad(metric, ((0, 0), (0, width - n_fit)))
-    sizes = (part // 3, part // 3, part // 6, part // 6)
+    sizes = (part // 3,) + (part // 6,) * 4
     parts = len(sizes)
-    four, two = sizes[0] * n_fit, sizes[2] * n_fit
-    late = 4 * four
+    four, two = sizes[0] * n_fit, sizes[1] * n_fit
+    late = 12 * two
     rows, panel = ao // n_orb, ao // n_aux
     dma = pltpu.SemaphoreType.DMA
     bf16, i16 = jnp.bfloat16, jnp.int16
-    piece = (panel // 4 + 16, panel)
+    block = (panel + 16, panel)
     return pl.pallas_call(
-        functools.partial(kernel, aux_local, sizes),
+        functools.partial(kernel, sizes),
         out_shape=jax.ShapeDtypeStruct((rows, panel), F32),
-        in_specs=[pl.BlockSpec(memory_space=pltpu.VMEM)] * 2,
-        out_specs=pl.BlockSpec(memory_space=pltpu.VMEM),
+        in_specs=[pl.BlockSpec(memory_space=pl.ANY)] + [pl.BlockSpec(memory_space=pltpu.VMEM)] * 2,
+        out_specs=pl.BlockSpec(memory_space=pl.ANY),
         scratch_shapes=[
+            pltpu.VMEM((aux_local, occ_local, ao), bf16),
+            pltpu.VMEM((n_aux, part * aux_local, ao), bf16),
+            pltpu.VMEM((aux_local * occ_local, aux_local * occ_local), bf16),
+            pltpu.VMEM((survive.shape[0], ao), F32),
+            pltpu.VMEM((aux_local, width), bf16),
             pltpu.VMEM((4, part * n_fit, ao), bf16),
             pltpu.VMEM((late, 3 * panel), bf16),
             pltpu.VMEM((panel, late), bf16),
@@ -491,20 +676,21 @@
             pltpu.VMEM((n_fit, width), bf16),
             pltpu.VMEM((four, four), bf16),
             pltpu.VMEM((two, two), bf16),
-            pltpu.VMEM((8, *piece), i16),
-            pltpu.VMEM((8, *piece), i16),
-            pltpu.VMEM((12, *piece), i16),
+            pltpu.VMEM((2, *block), i16),
+            pltpu.VMEM((2, *block), i16),
+            pltpu.VMEM((3, *block), i16),
+            dma((6,)),
             dma((4,)), dma((4,)),
             dma((4 * parts,)), dma((n_aux * parts,)),
-            dma((20 * parts,)), dma((32 * parts,)),
-            dma((8,)), dma((8,)),
-            dma((8,)), dma((12,)),
-            dma((2,)), dma((2,)),
+            dma((20 * parts,)), dma((24 * parts,)),
+            dma((12,)), dma((12,)),
+            dma((12,)), dma((18,)),
+            dma((6,)), dma((3,)),
         ],
         compiler_params=pltpu.CompilerParams(
             collective_id=0, has_side_effects=True, vmem_limit_bytes=66 * 1000 * 1000
         ),
-    )(blocks, metric)
+    )(half, metric, survive)
 
 
 def solution(mesh):

time: 175 us -> 161 us (0.920)
  Pallas kernels: 164 us -> 158 us
  local copies, waits for them, and re-layouts: 7.82 us -> 2.36 us
  other arithmetic: 3.48 us -> 0 us
    pallas_call x1, Pallas kernels: 164 us -> 158 us  [direct(): pl.pallas_call(functools.partial(kernel, sizes), out_shape=jax.ShapeDtype...]
    transpose x1 -> x0, local copies, waits for them, and re-layouts: 4.7 us -> none  [direct(): gated(half, survive).transpose(1, 0, 2).reshape(n_aux, part * aux_local, ao)]
    transpose x1 -> x0, other arithmetic: 2.8 us -> none  [direct(): gated(half, survive).transpose(1, 0, 2).reshape(n_aux, part * aux_local, ao)]
where the time goes in v4:
time: 161 us
  Pallas kernels  158 us (98%)
  local copies, waits for them, and re-layouts  2.36 us (1%)
    pallas_call x1, Pallas kernels, direct(): pl.pallas_call(functools.partial(kernel, sizes), out_shape=jax.ShapeDtype...  158 us

profile of v4, /device:TPU:0, one launch (start us, length us, event | category | flops | bytes accessed | tf_op | source)
XLA Modules:
  0.0 160.7 jit_solution(17509731829382286115)
XLA Ops:
  0.0 158.3 %shard_map.37 = f32[384,768]{1,0:T(8,128)} custom-call(bf16[16,48,3072]{2,1,0:T(8,128)(2,1)} %half_ref.1, bf16[16,64]{1,0:T(8,128)(2,1)} %metric_ref.1, s32[2,24]{1,0:T(2,128)} %bitcast.1), custom_call_target="tpu_custom_call" | custom-call | tf_op jit(solution)/shard_map/pallas_call | solution.py:660
  158.3 2.4 %copy.5 = f32[384,768]{1,0:T(8,128)} copy(f32[384,768]{1,0:T(8,128)} %shard_map.37) | data formatting | bytes 2359296

commit v5 on v4

--- a/solution.py
+++ b/solution.py
@@ -106,7 +106,6 @@
         )
     metric_pad[...] = jnp.zeros_like(metric_pad)
     metric_pad[:, pl.ds(0, metric_ref.shape[1])] = metric_ref[...]
-    pl.semaphore_wait(barrier, 8)
 
     def remote(src, dst, send, recv, a, o):
         return pltpu.make_async_remote_copy(
@@ -116,13 +115,6 @@
 
     def aligned(start, size, unit_of=128):
         return pl.ds(pl.multiple_of(start, unit_of), size)
-
-    metric_rows = aligned(z * aux_local, aux_local, aux_local)
-    gather = []
-    for d in (1, 3, 2):
-        copy = remote(metric_pad, whole.at[metric_rows], gs.at[d], gr.at[d], (z + d) % n_aux, orb)
-        copy.start()
-        gather.append(copy)
 
     def given_rows(q):
         return pl.ds(begins[q] * aux_local, sizes[q] * aux_local)
@@ -158,6 +150,14 @@
             )
 
     sort_rows(1 - side, True)
+    pl.semaphore_wait(barrier, 8)
+
+    metric_rows = aligned(z * aux_local, aux_local, aux_local)
+    gather = []
+    for d in (1, 3, 2):
+        copy = remote(metric_pad, whole.at[metric_rows], gs.at[d], gr.at[d], (z + d) % n_aux, orb)
+        copy.start()
+        gather.append(copy)
 
     @pl.when(end)
     def _():
@@ -167,8 +167,8 @@
     @pl.when(jnp.logical_not(end))
     def _():
         for r, q in (
-            (FAR_END, 0), (FAR_END, 1), (FAR_INNER, 0), (FAR_END, 2), (FAR_END, 3),
-            (FAR_END, 4), (FAR_INNER, 1), (FAR_INNER, 2), (FAR_INNER, 3), (FAR_INNER, 4),
+            (FAR_END, 0), (FAR_END, 1), (FAR_INNER, 0), (FAR_INNER, 1), (FAR_END, 2),
+            (FAR_END, 3), (FAR_END, 4), (FAR_INNER, 2), (FAR_INNER, 3), (FAR_INNER, 4),
         ):
             spread(r, q).start()
 
@@ -298,8 +298,8 @@
     def contract(p, tile, q, begin):
         at = aligned(tile, step)
         if q is None:
-            deep = fit_at[-1] + depth_of(parts - 1)
-            more = jnp.dot(left[...], fit[pl.ds(0, deep), at], preferred_element_type=F32)
+            late = pl.ds(fit_at[begin], fit_at[-1] + depth_of(parts - 1) - fit_at[begin])
+            more = jnp.dot(left[:, late], fit[late, at], preferred_element_type=F32)
         elif p:
             more = jnp.dot(
                 early[:, pl.ds(0, depth_of(q))], fit[pl.ds(fit_at[q], depth_of(q)), at],
@@ -310,7 +310,7 @@
                 left[:, pl.ds(fit_at[q], depth_of(q))], fit[pl.ds(fit_at[q], depth_of(q)), at],
                 preferred_element_type=F32,
             )
-        acc[p, :, at] = more if begin else acc[p, :, at] + more
+        acc[p, :, at] = more if begin is True else acc[p, :, at] + more
 
     def contract_all(p, q, begin):
         @pl.loop(0, 3)
@@ -390,7 +390,7 @@
     def _():
         for r, q in (
             (MATE, 0), (MATE, 1), (FAR_END, 0), (FAR_END, 1), (MATE, 2), (FAR_INNER, 0),
-            (MATE, 3), (MATE, 4),
+            (MATE, 3), (FAR_INNER, 1), (MATE, 4),
         ):
             arrive(r, q)
 
@@ -414,21 +414,24 @@
     def _():
         for q in (2, 3, 4):
             arrive(FAR_END, q)
-        arrive(FAR_INNER, 1)
-
-    arrive(FAR_INNER, 2)
+
     slots_of(1)
     fit_part(1)
     turn(1, 1)
     turn(0, 1)
     contract_all(1, 1, False)
+    contract_all(0, 1, False)
+    arrive(FAR_INNER, 2)
     arrive(FAR_INNER, 3)
-    contract_all(0, 1, False)
     slots_of(2)
     fit_part(2)
     turn(1, 2)
+    turn(0, 2)
+    contract(1, 0, 2, False)
+    contract(1, step, 2, False)
     arrive(FAR_INNER, 4)
-    contract_all(1, 2, False)
+    contract(1, 2 * step, 2, False)
+    contract(0, far_edge, 2, False)
     slots_of(3)
     fit_part(3)
     turn(1, 3)
@@ -452,7 +455,7 @@
     hold = jnp.logical_and(holder, jnp.logical_not(end))
     in_order = tuple((k, i) for k in (F, N) for i in range(pieces))
     mixed_order = (
-        (F, 0), (F, 1), (F, 2), (N, 0), (F, 3), (N, 1), (F, 4), (N, 2), (N, 3), (F, 5), (N, 4), (N, 5),
+        (F, 0), (F, 1), (F, 2), (N, 0), (F, 3), (N, 1), (F, 4), (N, 2), (F, 5), (N, 3), (N, 4), (N, 5),
     )
     hold_order = (
         (F, 0), (F, 1), (N, 0), (N, 1), (N, 2), (F, 2), (N, 3), (F, 3), (F, 4), (F, 5), (N, 4), (N, 5),
@@ -469,10 +472,10 @@
         for i in range(2, pieces):
             give(FAR, far_level, i)
 
-    for q in range(2, parts):
+    for q in range(3, parts):
         turn(0, q)
-    contract(0, far_edge, None, False)
-    contract(0, step, None, False)
+    contract(0, far_edge, None, 3)
+    contract(0, step, None, 2)
     far_top = tops_of(0, far)
 
     def along(k, i, into, there):
@@ -552,7 +555,7 @@
     def _():
         give_rest(in_order[pieces:])
 
-    contract(0, near_edge, None, False)
+    contract(0, near_edge, None, 2)
     near_top = tops_of(0, near)
 
     def near_pass(i, combined):

time: 161 us -> 159 us (0.988)
    pallas_call x1, Pallas kernels: 158 us -> 157 us  [direct(): pl.pallas_call(functools.partial(kernel, sizes), out_shape=jax.ShapeDtype...]
where the time goes in v5:
time: 159 us
  Pallas kernels  157 us (99%)
  local copies, waits for them, and re-layouts  2.36 us (1%)
    pallas_call x1, Pallas kernels, direct(): pl.pallas_call(functools.partial(kernel, sizes), out_shape=jax.ShapeDtype...  157 us

profile of v5, /device:TPU:0, one launch (start us, length us, event | category | flops | bytes accessed | tf_op | source)
XLA Modules:
  0.0 158.9 jit_solution(12803458884412828699)
XLA Ops:
  0.0 156.6 %shard_map.37 = f32[384,768]{1,0:T(8,128)} custom-call(bf16[16,48,3072]{2,1,0:T(8,128)(2,1)} %half_ref.1, bf16[16,64]{1,0:T(8,128)(2,1)} %metric_ref.1, s32[2,24]{1,0:T(2,128)} %bitcast.1), custom_call_target="tpu_custom_call" | custom-call | tf_op jit(solution)/shard_map/pallas_call | solution.py:663
  156.6 2.4 %copy.5 = f32[384,768]{1,0:T(8,128)} copy(f32[384,768]{1,0:T(8,128)} %shard_map.37) | data formatting | bytes 2359296

commit v6 on v5

--- a/solution.py
+++ b/solution.py
@@ -133,9 +133,10 @@
             zs.at[r * parts + q], zr.at[z * parts + q], there, orb,
         )
 
-    def sort_rows(pair, first):
-        span = count // 2
-        rows_at = pl.multiple_of(pair * span, span)
+    def sort_rows(dest, dests, first):
+        span = dests * count // n_aux
+        rows_at = pl.multiple_of(dest * (count // n_aux), count // n_aux)
+        pair = dest // 2
         for t in range(tiles):
             at = pl.ds(t * tile_width, tile_width)
             if first:
@@ -145,11 +146,11 @@
                 preferred_element_type=F32,
             )
             gated_rows = sorted_rows * gate[pl.ds(pair, 1), at]
-            m_ref[pl.ds(2 * pair, 2), :, at] = gated_rows.astype(m_ref.dtype).reshape(
-                2, span // 2, tile_width
+            m_ref[pl.ds(dest, dests), :, at] = gated_rows.astype(m_ref.dtype).reshape(
+                dests, count // n_aux, tile_width
             )
 
-    sort_rows(1 - side, True)
+    sort_rows(far_end, 1, True)
     pl.semaphore_wait(barrier, 8)
 
     metric_rows = aligned(z * aux_local, aux_local, aux_local)
@@ -166,13 +167,20 @@
 
     @pl.when(jnp.logical_not(end))
     def _():
+        for q in range(2):
+            spread(FAR_END, q).start()
+
+    sort_rows(far_inner, 1, False)
+
+    @pl.when(jnp.logical_not(end))
+    def _():
         for r, q in (
-            (FAR_END, 0), (FAR_END, 1), (FAR_INNER, 0), (FAR_INNER, 1), (FAR_END, 2),
-            (FAR_END, 3), (FAR_END, 4), (FAR_INNER, 2), (FAR_INNER, 3), (FAR_INNER, 4),
+            (FAR_INNER, 0), (FAR_INNER, 1), (FAR_END, 2), (FAR_END, 3), (FAR_END, 4),
+            (FAR_INNER, 2), (FAR_INNER, 3), (FAR_INNER, 4),
         ):
             spread(r, q).start()
 
-    sort_rows(side, False)
+    sort_rows(2 * side, 2, False)
 
     @pl.when(end)
     def _():

time: 159 us -> 158 us (level)
  no operation moved by 1% of the time
where the time goes in v6:
time: 158 us
  Pallas kernels  156 us (99%)
  local copies, waits for them, and re-layouts  2.36 us (1%)
    pallas_call x1, Pallas kernels, direct(): pl.pallas_call(functools.partial(kernel, sizes), out_shape=jax.ShapeDtype...  156 us

profile of v6, /device:TPU:0, one launch (start us, length us, event | category | flops | bytes accessed | tf_op | source)
XLA Modules:
  0.0 158.1 jit_solution(16837224620698279559)
XLA Ops:
  0.0 155.8 %shard_map.37 = f32[384,768]{1,0:T(8,128)} custom-call(bf16[16,48,3072]{2,1,0:T(8,128)(2,1)} %half_ref.1, bf16[16,64]{1,0:T(8,128)(2,1)} %metric_ref.1, s32[2,24]{1,0:T(2,128)} %bitcast.1), custom_call_target="tpu_custom_call" | custom-call | tf_op jit(solution)/shard_map/pallas_call | solution.py:671
  155.8 2.4 %copy.5 = f32[384,768]{1,0:T(8,128)} copy(f32[384,768]{1,0:T(8,128)} %shard_map.37) | data formatting | bytes 2359296
